TPU v7x, 512 devices: a whole 4x4x16 slice. The times are simulated.
512 devices in a mesh: panel: 8 (over x_lo, y), gx: 64 (over z, x_hi, core).
Axes of the slice: x: 4 (x_hi: 2, x_lo: 2; x = x_hi * 2 + x_lo), y: 4, z: 16, core: 2. Of those that a mesh axis runs over, the one named last changes fastest.
Arguments:
- right_side: float32 [20, 4096, 1024], P(None, 'gx', 'panel'), may hold values from -40 to 40
- previous: float32 [20, 4096, 1024], P(None, 'gx', 'panel'), may hold values from -1.8 to 1.8
- diagonal: float32 [20, 4096, 1024], P(None, 'gx', 'panel'), may hold values from 0.5 to 2
- vertical: float32 [19, 4096, 1024], P(None, 'gx', 'panel'), may hold values from 0.5 to 2
- metric_a: float32 [4096, 1024], P('gx', 'panel'), may hold values from 0.5 to 2
- metric_b: float32 [4096, 1024], P('gx', 'panel'), may hold values from 0.5 to 2
- profile: float32 [20], replicated, may hold values from 0.5 to 2
- column_inverse: bfloat16 [4, 20, 4096, 1024], P(None, None, 'gx', 'panel'), may hold values from -0.125 to 0.625, as said below
- edge_turn: int32 [4, 64, 8], replicated, may hold values from 0 to 3
Outputs:
- increment: float32 [20, 4096, 1024], P(None, 'gx', 'panel')
Inputs may be any that keep to these rules, and one draw needn't show every extreme that they name: Entry column_inverse[c, k] lies in row k mod 4, column c of the inverse of the block of 4 levels that holds level k. `edge_turn`: entries 0 and 2 are read only for their lowest bit; entries 1 and 3 reverse with the lowest bit and negate with the value 2 bit.
All inputs are finite; a program needn't handle non-finite values.
Results may differ from a plain program's by a relative error of at most 0.0003.
Values sent between devices are 32-bit elements; how exact they have to be, the bound alone decides.
No kernel may reach another device: no remote copies, remote signals or barrier semaphores. Data moves between devices by JAX's collectives and lax.ppermute only.
A program may use at most 64 MiB of HBM per device.

v0:
```python
import functools

import jax
import jax.numpy as jnp
from jax import lax
from jax.sharding import Mesh
from jax.sharding import PartitionSpec as P

BK = 4
GX = ("gx_0", "gx_1", "gx_2")
PANEL = ("panel_0", "panel_1")
PANEL_GX = ("panel_0", "panel_1", "gx_0", "gx_1", "gx_2")


def from_behind(block, axis, distance):
    devices = range(lax.axis_size(axis))
    route = [((i - distance) % len(devices), i) for i in devices]
    return lax.ppermute(block, axis, route)


def by_axis(shard, axes):
    return functools.reduce(lax.psum, axes, shard)


def flip_where(condition, values, dimension):
    return jnp.where(condition, jnp.flip(values, dimension), values)


def orient(values, code):
    turned = flip_where(code % 2 == 1, values, 1)
    return jnp.where(code // 2 == 1, -turned, turned)


def from_gx(values, offset):
    return from_behind(values, GX, offset)


def from_panel(values, offset):
    return from_behind(values, PANEL, offset)


def assemble(pressure, diagonal, vertical, flux_a, flux_b, high_a, high_b):
    next_a = jnp.concatenate([flux_a[:, 1:], high_a[:, None]], axis=1)
    next_b = jnp.concatenate([flux_b[:, :, 1:], high_b[:, :, None]], axis=2)
    vertical_flux = vertical * (pressure[1:] - pressure[:-1])
    zeros_row = jnp.zeros((1,) + pressure.shape[1:], jnp.float32)
    upward = jnp.concatenate([zeros_row, vertical_flux], axis=0) - jnp.concatenate(
        [vertical_flux, zeros_row], axis=0
    )
    return diagonal * pressure + (flux_a - next_a + flux_b - next_b) + upward


def local_fluxes(pressure, low_a, low_b, face_a, face_b):
    prev_a = jnp.concatenate([low_a[:, None], pressure[:, :-1]], axis=1)
    prev_b = jnp.concatenate([low_b[:, :, None], pressure[:, :, :-1]], axis=2)
    return (face_a * (pressure - prev_a), face_b * (pressure - prev_b))


def precondition(resid, column_inverse):
    level_count, rows_here, cols_here = resid.shape
    blocks = resid.reshape(level_count // BK, BK, rows_here, cols_here)
    inverse = column_inverse.reshape(BK, level_count // BK, BK, rows_here, cols_here)
    result = inverse[0].astype(jnp.float32) * blocks[:, 0:1]
    for column in range(1, BK):
        result = result + inverse[column].astype(jnp.float32) * blocks[:, column : column + 1]
    return result.reshape(level_count, rows_here, cols_here)


def shards(
    right_side, previous, diagonal, vertical, metric_a, metric_b, profile, column_inverse, edge_turn
):
    gx_index = lax.axis_index(GX)
    panel_index = lax.axis_index(PANEL)
    turns = edge_turn[:, gx_index, panel_index]
    face_a = metric_a[None] * profile[:, None, None]
    face_b = metric_b[None] * profile[:, None, None]

    def operate(pressure):
        low_a = flip_where(turns[0] % 2 == 1, from_gx(pressure[:, -1], 1), 1)
        low_b = flip_where(turns[2] % 2 == 1, from_panel(pressure[:, :, -1], 1), 1)
        flux_a, flux_b = local_fluxes(pressure, low_a, low_b, face_a, face_b)
        high_a = orient(from_gx(flux_a[:, 0], -1), turns[1])
        high_b = orient(from_panel(flux_b[:, :, 0], -1), turns[3])
        return assemble(pressure, diagonal, vertical, flux_a, flux_b, high_a, high_b)

    resid_first = right_side - operate(previous)
    search_first = precondition(resid_first, column_inverse)
    image_first = operate(search_first)
    cross_first, square_first = (
        by_axis(jnp.sum(resid_first * image_first), PANEL_GX),
        by_axis(jnp.sum(image_first * image_first), PANEL_GX),
    )
    alpha_first = cross_first / square_first
    resid_second = resid_first - alpha_first * image_first
    search_second = precondition(resid_second, column_inverse)
    image_second = operate(search_second)
    along_first, image_square, resid_image, resid_along = (
        by_axis(jnp.sum(image_second * image_first), PANEL_GX),
        by_axis(jnp.sum(image_second * image_second), PANEL_GX),
        by_axis(jnp.sum(resid_second * image_second), PANEL_GX),
        by_axis(jnp.sum(resid_second * image_first), PANEL_GX),
    )
    beta_coef = along_first / square_first
    alpha_second = (resid_image - beta_coef * resid_along) / (
        image_square - 2.0 * beta_coef * along_first + beta_coef * beta_coef * square_first
    )
    direction = search_second - beta_coef * search_first
    return alpha_first * search_first + alpha_second * direction


def solution(mesh):
    finer = Mesh(
        mesh.devices.reshape(2, 4, 16, 2, 2), ("panel_0", "panel_1", "gx_0", "gx_1", "gx_2")
    )
    in_specs = (
        P(None, GX, PANEL),
        P(None, GX, PANEL),
        P(None, GX, PANEL),
        P(None, GX, PANEL),
        P(GX, PANEL),
        P(GX, PANEL),
        P(),
        P(None, None, GX, PANEL),
        P(),
    )
    out_specs = P(None, GX, PANEL)
    return jax.shard_map(
        shards, mesh=finer, in_specs=in_specs, out_specs=out_specs, check_vma=False
    )
```

profile of v0, /device:TPU:1, one launch (start us, length us, event | category | flops | bytes accessed | tf_op | source)
XLA Modules:
  0.0 240.2 jit_solution(17056232726374985012)
XLA Ops:
  1.7 4.0 %collective-permute-start.2 = (f32[20,64]{1,0:T(8,128)S(1)}, f32[20,64]{1,0:T(8,128)S(1)}, u32[]{:S(2)}, u32[]{:S(2)}) collective-permute-start(f32[20,64]{1,0:T(8,128)S(1)} %bitcast.126), channel_id=1, source_target_pairs={{448,0},{0,64},{64,128},{128,192},{192,256},{256,320},{320,384},{3... | collective-permute-start | bytes 15368 | tf_op jit(solution)/shard_map/ppermute | solution.py:18
  6.1 5.5 %collective-permute-start = (f32[20,128]{1,0:T(8,128)S(1)}, f32[20,128]{1,0:T(8,128)S(1)}, u32[]{:S(2)}, u32[]{:S(2)}) collective-permute-start(f32[20,128]{1,0:T(8,128)S(1)} %slice_bitcast_fusion.13), channel_id=1, source_target_pairs={{63,0},{0,1},{1,2},{2,3},{3,4},{4,5},{5,6},{6,7},{7,8},{8,9},{9,10... | collective-permute-start | bytes 30728 | tf_op jit(solution)/shard_map/ppermute | solution.py:18
  28.6 3.6 %collective-permute-start.3 = (f32[20,64]{1,0:T(8,128)S(1)}, f32[20,64]{1,0:T(8,128)S(1)}, u32[]{:S(2)}, u32[]{:S(2)}) collective-permute-start(f32[20,64]{1,0:T(8,128)S(1)} %bitcast.122), channel_id=1, source_target_pairs={{64,0},{128,64},{192,128},{256,192},{320,256},{384,320},{448,384},... | collective-permute-start | bytes 15368 | tf_op jit(solution)/shard_map/ppermute | solution.py:18
  34.3 5.5 %collective-permute-start.1 = (f32[20,128]{1,0:T(8,128)S(1)}, f32[20,128]{1,0:T(8,128)S(1)}, u32[]{:S(2)}, u32[]{:S(2)}) collective-permute-start(f32[20,128]{1,0:T(8,128)S(1)} %slice_bitcast_fusion.12), channel_id=1, source_target_pairs={{1,0},{2,1},{3,2},{4,3},{5,4},{6,5},{7,6},{8,7},{9,8},{10,9},{11,1... | collective-permute-start | bytes 30728 | tf_op jit(solution)/shard_map/ppermute | solution.py:18
  41.3 3.8 %fusion.2 = f32[20,64,128]{2,0,1:T(8,128)S(1)} fusion(f32[20,64,128]{2,1,0:T(8,128)} %param.11, f32[20,64,128]{2,0,1:T(8,128)S(1)} %get-tuple-element.51, f32[20,64,128]{2,0,1:T(8,128)S(1)} %get-tuple-element.50, f32[20,1,128]{2,0,1:T(8,128)S(1)} %fusion.19, f32[20,63,128]{2,0,1:T(8,128)} %slice.206, f32[20,64,1]{2,0,1:T(8,128)} %copy.381, ...), kind=kLoop, calls=%fused_computation.22 | loop fusion | flops 1638400 | bytes 5865472 | tf_op jit(solution)/shard_map/sub | solution.py:86
  58.5 3.3 %collective-permute-done.4 = f32[20,128]{1,0:T(8,128)S(1)} collective-permute-done((f32[20,128]{1,0:T(8,128)S(1)}, f32[20,128]{1,0:T(8,128)S(1)}, u32[]{:S(2)}, u32[]{:S(2)}) %collective-permute-start.4) | collective-permute-done | bytes 10272 | tf_op jit(solution)/shard_map/ppermute | solution.py:18
  64.5 5.7 %collective-permute-start.7 = (f32[20,64]{1,0:T(8,128)}, f32[20,64]{1,0:T(8,128)}, u32[]{:S(2)}, u32[]{:S(2)}) collective-permute-start(f32[20,64]{1,0:T(8,128)} %bitcast.31), channel_id=1, source_target_pairs={{64,0},{128,64},{192,128},{256,192},{320,256},{384,320},{448,384},... | collective-permute-start | bytes 15368 | tf_op jit(solution)/shard_map/ppermute | solution.py:18
  72.9 8.2 %collective-permute-start.5 = (f32[20,128]{1,0:T(8,128)}, f32[20,128]{1,0:T(8,128)S(1)}, u32[]{:S(2)}, u32[]{:S(2)}) collective-permute-start(f32[20,128]{1,0:T(8,128)} %slice_bitcast_fusion.10), channel_id=1, source_target_pairs={{1,0},{2,1},{3,2},{4,3},{5,4},{6,5},{7,6},{8,7},{9,8},{10,9},{11,1... | collective-permute-start | bytes 30728 | tf_op jit(solution)/shard_map/ppermute | solution.py:18
  83.3 3.9 %multiply_reduce_fusion.4 = (f32[]{:T(128)}, f32[]{:T(128)}, f32[20,64,128]{2,0,1:T(8,128)S(1)}) fusion(f32[20,64,128]{2,0,1:T(8,128)S(1)} %fusion.2, f32[19,64,128]{2,0,1:T(8,128)} %copy_multiply_fusion.1, f32[20,64,1]{2,0,1:T(8,128)} %copy.399, f32[20,64,127]{2,0,1:T(8,128)} %slice.223, f32[20,64,128]{2,0,1:T(8,128)S(1)} %get-tuple-element.49, ...), kind=kLoop, calls=%fused_computation.57 | loop fusion | flops 2129918 | bytes 5865480 | tf_op jit(solution)/shard_map/reduce_sum | solution.py:91
  87.2 4.5 %all-reduce.15 = (f32[]{:T(128)}, f32[]{:T(128)}) all-reduce(f32[]{:T(128)} %get-tuple-element.10, f32[]{:T(128)} %get-tuple-element.9), channel_id=1, replica_groups=mesh['panel_0'=2,'panel_1'=4,'gx_0'=16,'gx_1'=2,'gx_2'=2] {'panel_0'}, use_global_device_ids=true, to_apply=%region_1.2 | all-reduce | flops 2 | bytes 16 | tf_op jit(solution)/shard_map/psum | solution.py:22
  91.7 6.7 %all-reduce.9 = (f32[]{:T(128)}, f32[]{:T(128)}) all-reduce(f32[]{:T(128)} %get-tuple-element.39, f32[]{:T(128)} %get-tuple-element.40), channel_id=1, replica_groups=mesh['panel_0'=2,'panel_1'=4,'gx_0'=16,'gx_1'=2,'gx_2'=2] {'panel_1'}, use_global_device_ids=true, to_apply=%region_2.3 | all-reduce | flops 2 | bytes 16 | tf_op jit(solution)/shard_map/psum | solution.py:22
  98.4 22.8 %all-reduce.7 = (f32[]{:T(128)}, f32[]{:T(128)}) all-reduce(f32[]{:T(128)} %get-tuple-element.21, f32[]{:T(128)} %get-tuple-element.22), channel_id=1, replica_groups=mesh['panel_0'=2,'panel_1'=4,'gx_0'=16,'gx_1'=2,'gx_2'=2] {'gx_0'}, use_global_device_ids=true, to_apply=%region_3.4 | all-reduce | flops 2 | bytes 16 | tf_op jit(solution)/shard_map/psum | solution.py:22
  121.1 7.0 %all-reduce.13 = (f32[]{:T(128)}, f32[]{:T(128)}) all-reduce(f32[]{:T(128)} %get-tuple-element.15, f32[]{:T(128)} %get-tuple-element.16), channel_id=1, replica_groups=mesh['panel_0'=2,'panel_1'=4,'gx_0'=16,'gx_1'=2,'gx_2'=2] {'gx_1'}, use_global_device_ids=true, to_apply=%region_4.5 | all-reduce | flops 2 | bytes 16 | tf_op jit(solution)/shard_map/psum | solution.py:22
  128.2 13.9 %all-reduce.11 = (f32[]{:T(128)}, f32[]{:T(128)}) all-reduce(f32[]{:T(128)} %get-tuple-element.33, f32[]{:T(128)} %get-tuple-element.34), channel_id=1, replica_groups=mesh['panel_0'=2,'panel_1'=4,'gx_0'=16,'gx_1'=2,'gx_2'=2] {'gx_2'}, use_global_device_ids=true, to_apply=%region_5.6 | all-reduce | flops 2 | bytes 16 | tf_op jit(solution)/shard_map/psum | solution.py:22
  153.2 3.2 %collective-permute-start.8 = (f32[20,128]{1,0:T(8,128)S(1)}, f32[20,128]{1,0:T(8,128)S(1)}, u32[]{:S(2)}, u32[]{:S(2)}) collective-permute-start(f32[20,128]{1,0:T(8,128)S(1)} %slice_bitcast_fusion.9), channel_id=1, source_target_pairs={{63,0},{0,1},{1,2},{2,3},{3,4},{4,5},{5,6},{6,7},{7,8},{8,9},{9,10... | collective-permute-start | bytes 30728 | tf_op jit(solution)/shard_map/ppermute | solution.py:18
  157.8 2.6 %multiply_multiply_fusion.3 = (f32[20,64,128]{2,0,1:T(8,128)}, f32[20,64,128]{2,0,1:T(8,128)S(1)}) fusion(f32[20,64,128]{2,0,1:T(8,128)S(1)} %fusion.12, f32[20,63,128]{2,0,1:T(8,128)} %slice.232, f32[20,1,128]{2,0,1:T(8,128)S(1)} %select_bitcast_fusion.1, f32[20]{0:T(128)S(1)} %copy-done.15, f32[64,128]{1,0:T(8,128)S(1)} %copy-done.13, ...), kind=kLoop, calls=%fused_computation.3 | loop fusion | flops 1310720 | bytes 3342416 | tf_op jit(solution)/shard_map/mul | solution.py:56
  160.7 4.9 %collective-permute-start.11 = (f32[20,64]{1,0:T(8,128)S(1)}, f32[20,64]{1,0:T(8,128)S(1)}, u32[]{:S(2)}, u32[]{:S(2)}) collective-permute-start(f32[20,64]{1,0:T(8,128)S(1)} %bitcast.123), channel_id=1, source_target_pairs={{64,0},{128,64},{192,128},{256,192},{320,256},{384,320},{448,384},... | collective-permute-start | bytes 15368 | tf_op jit(solution)/shard_map/ppermute | solution.py:18
  169.5 6.8 %collective-permute-start.9 = (f32[20,128]{1,0:T(8,128)S(1)}, f32[20,128]{1,0:T(8,128)S(1)}, u32[]{:S(2)}, u32[]{:S(2)}) collective-permute-start(f32[20,128]{1,0:T(8,128)S(1)} %slice_bitcast_fusion.8), channel_id=1, source_target_pairs={{1,0},{2,1},{3,2},{4,3},{5,4},{6,5},{7,6},{8,7},{9,8},{10,9},{11,1... | collective-permute-start | bytes 30728 | tf_op jit(solution)/shard_map/ppermute | solution.py:18
  177.7 4.3 %multiply_reduce_fusion = (f32[]{:T(128)}, f32[]{:T(128)}, f32[]{:T(128)}, f32[]{:T(128)}) fusion(f32[20,64,128]{2,0,1:T(8,128)S(1)} %get-tuple-element.41, f32[20,64,128]{2,0,1:T(8,128)} %copy-done.2, f32[19,64,128]{2,0,1:T(8,128)} %copy_multiply_fusion, f32[20,64,1]{2,0,1:T(8,128)} %copy.410, f32[20,64,127]{2,0,1:T(8,128)} %slice.237, ...), kind=kLoop, calls=%fused_computation.52 | loop fusion | flops 2785276 | bytes 5865488 | tf_op jit(solution)/shard_map/reduce_sum | solution.py:99
  182.0 4.5 %all-reduce.14 = (f32[]{:T(128)}, f32[]{:T(128)}, f32[]{:T(128)}, f32[]{:T(128)}) all-reduce(f32[]{:T(128)} %get-tuple-element.6, f32[]{:T(128)} %get-tuple-element.8, f32[]{:T(128)} %get-tuple-element.7, f32[]{:T(128)} %get-tuple-element.5), channel_id=1, replica_groups=mesh['panel_0'=2,'panel_1'=4,'gx_0'=16,'gx_1'=2,'gx_2'=2] {'panel_0'}, use_global_device_ids=true, to_apply=%region_19.20 | all-reduce | flops 4 | bytes 32 | tf_op jit(solution)/shard_map/psum | solution.py:22
  186.4 6.7 %all-reduce.8 = (f32[]{:T(128)}, f32[]{:T(128)}, f32[]{:T(128)}, f32[]{:T(128)}) all-reduce(f32[]{:T(128)} %get-tuple-element.35, f32[]{:T(128)} %get-tuple-element.36, f32[]{:T(128)} %get-tuple-element.37, f32[]{:T(128)} %get-tuple-element.38), channel_id=1, replica_groups=mesh['panel_0'=2,'panel_1'=4,'gx_0'=16,'gx_1'=2,'gx_2'=2] {'panel_1'}, use_global_device_ids=true, to_apply=%region_20.21 | all-reduce | flops 4 | bytes 32 | tf_op jit(solution)/shard_map/psum | solution.py:22
  193.1 21.4 %all-reduce.6 = (f32[]{:T(128)}, f32[]{:T(128)}, f32[]{:T(128)}, f32[]{:T(128)}) all-reduce(f32[]{:T(128)} %get-tuple-element.17, f32[]{:T(128)} %get-tuple-element.18, f32[]{:T(128)} %get-tuple-element.19, f32[]{:T(128)} %get-tuple-element.20), channel_id=1, replica_groups=mesh['panel_0'=2,'panel_1'=4,'gx_0'=16,'gx_1'=2,'gx_2'=2] {'gx_0'}, use_global_device_ids=true, to_apply=%region_21.22 | all-reduce | flops 4 | bytes 32 | tf_op jit(solution)/shard_map/psum | solution.py:22
  214.5 8.0 %all-reduce.12 = (f32[]{:T(128)}, f32[]{:T(128)}, f32[]{:T(128)}, f32[]{:T(128)}) all-reduce(f32[]{:T(128)} %get-tuple-element.11, f32[]{:T(128)} %get-tuple-element.12, f32[]{:T(128)} %get-tuple-element.13, f32[]{:T(128)} %get-tuple-element.14), channel_id=1, replica_groups=mesh['panel_0'=2,'panel_1'=4,'gx_0'=16,'gx_1'=2,'gx_2'=2] {'gx_1'}, use_global_device_ids=true, to_apply=%region_22.23 | all-reduce | flops 4 | bytes 32 | tf_op jit(solution)/shard_map/psum | solution.py:22
  222.4 12.2 %all-reduce.10 = (f32[]{:T(128)}, f32[]{:T(128)}, f32[]{:T(128)}, f32[]{:T(128)}) all-reduce(f32[]{:T(128)} %get-tuple-element.29, f32[]{:T(128)} %get-tuple-element.30, f32[]{:T(128)} %get-tuple-element.31, f32[]{:T(128)} %get-tuple-element.32), channel_id=1, replica_groups=mesh['panel_0'=2,'panel_1'=4,'gx_0'=16,'gx_1'=2,'gx_2'=2] {'gx_2'}, use_global_device_ids=true, to_apply=%region_23.24 | all-reduce | flops 4 | bytes 32 | tf_op jit(solution)/shard_map/psum | solution.py:22
  (125 shorter events, 52.5 us)
Async XLA Ops:
  0.0 5.7 %copy-start = (f32[20,64,128]{2,1,0:T(8,128)S(1)}, f32[20,64,128]{2,1,0:T(8,128)}, u32[]{:S(2)}) copy-start(f32[20,64,128]{2,1,0:T(8,128)} %param.10) | copy-start | bytes 1966084
  1.4 10.3 %copy-start.3 = (f32[19,64,128]{2,1,0:T(8,128)S(1)}, f32[19,64,128]{2,1,0:T(8,128)}, u32[]{:S(2)}) copy-start(f32[19,64,128]{2,1,0:T(8,128)} %param.12) | copy-start | bytes 1867780
  1.7 23.2 %collective-permute-start.2 = (f32[20,64]{1,0:T(8,128)S(1)}, f32[20,64]{1,0:T(8,128)S(1)}, u32[]{:S(2)}, u32[]{:S(2)}) collective-permute-start(f32[20,64]{1,0:T(8,128)S(1)} %bitcast.126), channel_id=1, source_target_pairs={{448,0},{0,64},{64,128},{128,192},{192,256},{256,320},{320,384},{3... | collective-permute-start | bytes 15368 | tf_op jit(solution)/shard_map/ppermute | solution.py:18
  6.1 20.1 %collective-permute-start = (f32[20,128]{1,0:T(8,128)S(1)}, f32[20,128]{1,0:T(8,128)S(1)}, u32[]{:S(2)}, u32[]{:S(2)}) collective-permute-start(f32[20,128]{1,0:T(8,128)S(1)} %slice_bitcast_fusion.13), channel_id=1, source_target_pairs={{63,0},{0,1},{1,2},{2,3},{3,4},{4,5},{5,6},{6,7},{7,8},{8,9},{9,10... | collective-permute-start | bytes 30728 | tf_op jit(solution)/shard_map/ppermute | solution.py:18
  11.7 1.3 copy-start.12
  15.3 11.0 %copy-start.13 = (f32[64,128]{1,0:T(8,128)S(1)}, f32[64,128]{1,0:T(8,128)}, u32[]{:S(2)}) copy-start(f32[64,128]{1,0:T(8,128)} %param.13) | copy-start | bytes 98308
  15.3 11.0 %copy-start.14 = (f32[64,128]{1,0:T(8,128)S(1)}, f32[64,128]{1,0:T(8,128)}, u32[]{:S(2)}) copy-start(f32[64,128]{1,0:T(8,128)} %param.14) | copy-start | bytes 98308
  15.3 11.0 %copy-start.15 = (f32[20]{0:T(128)S(1)}, f32[20]{0:T(128)}, u32[]{:S(2)}) copy-start(f32[20]{0:T(128)} %param.15) | copy-start | bytes 244
  28.6 11.2 %collective-permute-start.3 = (f32[20,64]{1,0:T(8,128)S(1)}, f32[20,64]{1,0:T(8,128)S(1)}, u32[]{:S(2)}, u32[]{:S(2)}) collective-permute-start(f32[20,64]{1,0:T(8,128)S(1)} %bitcast.122), channel_id=1, source_target_pairs={{64,0},{128,64},{192,128},{256,192},{320,256},{384,320},{448,384},... | collective-permute-start | bytes 15368 | tf_op jit(solution)/shard_map/ppermute | solution.py:18
  34.3 6.9 %collective-permute-start.1 = (f32[20,128]{1,0:T(8,128)S(1)}, f32[20,128]{1,0:T(8,128)S(1)}, u32[]{:S(2)}, u32[]{:S(2)}) collective-permute-start(f32[20,128]{1,0:T(8,128)S(1)} %slice_bitcast_fusion.12), channel_id=1, source_target_pairs={{1,0},{2,1},{3,2},{4,3},{5,4},{6,5},{7,6},{8,7},{9,8},{10,9},{11,1... | collective-permute-start | bytes 30728 | tf_op jit(solution)/shard_map/ppermute | solution.py:18
  45.4 1.1 copy-start.8
  45.4 1.2 copy-start.10
  46.6 2.1 copy-start.4
  50.6 6.6 %collective-permute-start.6 = (f32[20,64]{1,0:T(8,128)S(1)}, f32[20,64]{1,0:T(8,128)S(1)}, u32[]{:S(2)}, u32[]{:S(2)}) collective-permute-start(f32[20,64]{1,0:T(8,128)S(1)} %bitcast.124), channel_id=1, source_target_pairs={{448,0},{0,64},{64,128},{128,192},{192,256},{256,320},{320,384},{3... | collective-permute-start | bytes 15368 | tf_op jit(solution)/shard_map/ppermute | solution.py:18
  53.5 8.3 %collective-permute-start.4 = (f32[20,128]{1,0:T(8,128)S(1)}, f32[20,128]{1,0:T(8,128)S(1)}, u32[]{:S(2)}, u32[]{:S(2)}) collective-permute-start(f32[20,128]{1,0:T(8,128)S(1)} %slice_bitcast_fusion.11), channel_id=1, source_target_pairs={{63,0},{0,1},{1,2},{2,3},{3,4},{4,5},{5,6},{6,7},{7,8},{8,9},{9,10... | collective-permute-start | bytes 30728 | tf_op jit(solution)/shard_map/ppermute | solution.py:18
  63.6 9.3 %copy-start.1 = (f32[20,64,128]{2,0,1:T(8,128)}, f32[20,64,128]{2,0,1:T(8,128)S(1)}, u32[]{:S(2)}) copy-start(f32[20,64,128]{2,0,1:T(8,128)S(1)} %get-tuple-element.48) | copy-start | bytes 1966084
  64.5 16.7 %collective-permute-start.7 = (f32[20,64]{1,0:T(8,128)}, f32[20,64]{1,0:T(8,128)}, u32[]{:S(2)}, u32[]{:S(2)}) collective-permute-start(f32[20,64]{1,0:T(8,128)} %bitcast.31), channel_id=1, source_target_pairs={{64,0},{128,64},{192,128},{256,192},{320,256},{384,320},{448,384},... | collective-permute-start | bytes 15368 | tf_op jit(solution)/shard_map/ppermute | solution.py:18
  72.9 10.3 %collective-permute-start.5 = (f32[20,128]{1,0:T(8,128)}, f32[20,128]{1,0:T(8,128)S(1)}, u32[]{:S(2)}, u32[]{:S(2)}) collective-permute-start(f32[20,128]{1,0:T(8,128)} %slice_bitcast_fusion.10), channel_id=1, source_target_pairs={{1,0},{2,1},{3,2},{4,3},{5,4},{6,5},{7,6},{8,7},{9,8},{10,9},{11,1... | collective-permute-start | bytes 30728 | tf_op jit(solution)/shard_map/ppermute | solution.py:18
  144.3 1.2 copy-start.11
  145.5 2.1 copy-start.5
  149.6 6.8 %collective-permute-start.10 = (f32[20,64]{1,0:T(8,128)S(1)}, f32[20,64]{1,0:T(8,128)S(1)}, u32[]{:S(2)}, u32[]{:S(2)}) collective-permute-start(f32[20,64]{1,0:T(8,128)S(1)} %bitcast.125), channel_id=1, source_target_pairs={{448,0},{0,64},{64,128},{128,192},{192,256},{256,320},{320,384},{3... | collective-permute-start | bytes 15368 | tf_op jit(solution)/shard_map/ppermute | solution.py:18
  153.2 4.6 %collective-permute-start.8 = (f32[20,128]{1,0:T(8,128)S(1)}, f32[20,128]{1,0:T(8,128)S(1)}, u32[]{:S(2)}, u32[]{:S(2)}) collective-permute-start(f32[20,128]{1,0:T(8,128)S(1)} %slice_bitcast_fusion.9), channel_id=1, source_target_pairs={{63,0},{0,1},{1,2},{2,3},{3,4},{4,5},{5,6},{6,7},{7,8},{8,9},{9,10... | collective-permute-start | bytes 30728 | tf_op jit(solution)/shard_map/ppermute | solution.py:18
  160.7 15.6 %collective-permute-start.11 = (f32[20,64]{1,0:T(8,128)S(1)}, f32[20,64]{1,0:T(8,128)S(1)}, u32[]{:S(2)}, u32[]{:S(2)}) collective-permute-start(f32[20,64]{1,0:T(8,128)S(1)} %bitcast.123), channel_id=1, source_target_pairs={{64,0},{128,64},{192,128},{256,192},{320,256},{384,320},{448,384},... | collective-permute-start | bytes 15368 | tf_op jit(solution)/shard_map/ppermute | solution.py:18
  169.5 8.1 %collective-permute-start.9 = (f32[20,128]{1,0:T(8,128)S(1)}, f32[20,128]{1,0:T(8,128)S(1)}, u32[]{:S(2)}, u32[]{:S(2)}) collective-permute-start(f32[20,128]{1,0:T(8,128)S(1)} %slice_bitcast_fusion.8), channel_id=1, source_target_pairs={{1,0},{2,1},{3,2},{4,3},{5,4},{6,5},{7,6},{8,7},{9,8},{10,9},{11,1... | collective-permute-start | bytes 30728 | tf_op jit(solution)/shard_map/ppermute | solution.py:18
  (4 other events, 3.9 us)
where the time goes:
time: 242 us; the launch traced here: 240 us
  blocking collectives  108 us (45%)
  starting transfers between devices  53.9 us (22%)
  local copies, waits for them, and re-layouts  32 us (13%)
  other arithmetic  26.9 us (11%)
  between operations  14.7 us (6%)
  waiting for transfers between devices  5.07 us (2%)
    psum x10, blocking collectives, by_axis(): return functools.reduce(lax.psum, axes, shard)  108 us
    ppermute x12, starting transfers between devices, from_behind(): return lax.ppermute(block, axis, route)  53.9 us
    mul x3, other arithmetic, local_fluxes(): return (face_a * (pressure - prev_a), face_b * (pressure - prev_b))  6.3 us
    ppermute x12, waiting for transfers between devices, from_behind(): return lax.ppermute(block, axis, route)  5.07 us
  transfers between devices with their start and end apart: 12, of which 2 were waited for; matrix products, arithmetic and copies ran while one was open for 10% of the time, Pallas kernels for 0%

commit v1 on v0

v1 whole, which is shorter than its diff:
```python
import jax
import jax.numpy as jnp
from jax import lax
from jax.experimental import pallas as pl
from jax.experimental.pallas import tpu as pltpu
from jax.sharding import Mesh
from jax.sharding import PartitionSpec as P

BK = 4
SHAPE = (2, 4, 16, 2, 2)
GX = ("gx_0", "gx_1", "gx_2")
PANEL = ("panel_0", "panel_1")
PLANE = ("panel_0", "panel_1", "gx_1", "gx_2")
COLUMN = ("gx_0",)
ROWS = 24
METRIC = 20
F32 = jnp.float32
VMEM = pl.BlockSpec(memory_space=pltpu.VMEM)


def reverse_lanes(values, length):
    lane = lax.broadcasted_iota(jnp.int32, values.shape, 1)
    index = jnp.where(lane < length, length - 1 - lane, lane)
    return jnp.take_along_axis(values, index, axis=1)


def reverse_rows(values):
    count = values.shape[0] // 8
    row = lax.broadcasted_iota(jnp.int32, (8, 128), 0)
    parts = [
        jnp.take_along_axis(values[8 * i : 8 * i + 8], 7 - row, axis=0)
        for i in reversed(range(count))
    ]
    return jnp.concatenate(parts, axis=0)


def flag(flags_ref, at):
    return flags_ref[at : at + 1, :]


def pack(field_ref, flags_ref, row_up, row_down, col_up, col_down, metrics=None):
    levels, height, width = field_ref.shape
    lane = lax.broadcasted_iota(jnp.int32, (height, width), 1)
    for k in range(levels):
        row_up[k : k + 1, :] = field_ref[k, height - 1 : height, :]
        row_down[k : k + 1, :] = field_ref[k, 0:1, :]
    for k in range(levels, ROWS):
        row_up[k : k + 1, :] = jnp.zeros((1, width), F32)
        row_down[k : k + 1, :] = jnp.zeros((1, width), F32)
    last = jnp.zeros((height, width), F32)
    first = jnp.zeros((height, width), F32)
    for k in range(levels):
        values = field_ref[k]
        last = jnp.where(lane == k, pltpu.roll(values, (k + 1) % width, 1), last)
        first = jnp.where(lane == k, pltpu.roll(values, k, 1) if k else values, first)
    if metrics is not None:
        metric_a, metric_b = metrics
        row_down[METRIC : METRIC + 1, :] = metric_a[0:1, :]
        first = jnp.where(lane == METRIC, pltpu.roll(metric_b[...], METRIC, 1), first)
    up, down = row_up[...], row_down[...]
    row_up[...] = jnp.where(flag(flags_ref, 0) > 0.5, reverse_lanes(up, width), up)
    row_down[...] = jnp.where(flag(flags_ref, 1) > 0.5, reverse_lanes(down, width), down)
    col_up[...] = jnp.where(flag(flags_ref, 2) > 0.5, reverse_rows(last), last)
    col_down[...] = jnp.where(flag(flags_ref, 3) > 0.5, reverse_rows(first), first)


def apply_operator(field_ref, coef, halo, flux_ref, emit):
    diagonal, vertical, metric_a, metric_b, spread, lanes, flags_ref = coef
    low_row, high_row, low_col, high_col, sent_row, sent_col, metric_row, metric_col = halo
    levels, height, width = field_ref.shape
    row = lax.broadcasted_iota(jnp.int32, (height, width), 0)
    lane = lax.broadcasted_iota(jnp.int32, (height, width), 1)
    own_row = sent_row[...]
    own_row = jnp.where(flag(flags_ref, 4) > 0.5, reverse_lanes(own_row, width), own_row)
    face_row = metric_row[METRIC : METRIC + 1, :] * spread[...]
    flux_ref[...] = flag(flags_ref, 5) * (face_row * (high_row[...] - own_row))
    own_col = sent_col[...]
    own_col = jnp.where(flag(flags_ref, 6) > 0.5, reverse_rows(own_col), own_col)
    face_col = metric_col[:, METRIC : METRIC + 1] * lanes[0:1, :]
    flux_col = flag(flags_ref, 7) * (face_col * (high_col[...] - own_col))
    below = None
    for k in range(levels):
        here = field_ref[k]
        scale = spread[k : k + 1, :]
        face_a = metric_a[...] * scale
        face_b = metric_b[...] * scale
        prev_a = jnp.where(row == 0, low_row[k : k + 1, :], pltpu.roll(here, 1, 0))
        edge = low_col[...]
        edge = pltpu.roll(edge, width - k, 1) if k else edge
        prev_b = jnp.where(lane == 0, edge, pltpu.roll(here, 1, 1))
        flux_a = face_a * (here - prev_a)
        flux_b = face_b * (here - prev_b)
        next_a = jnp.where(
            row == height - 1, flux_ref[k : k + 1, :], pltpu.roll(flux_a, height - 1, 0)
        )
        next_b = jnp.where(
            lane == width - 1,
            pltpu.roll(flux_col, width - 1 - k, 1),
            pltpu.roll(flux_b, width - 1, 1),
        )
        total = diagonal[k] * here + (flux_a - next_a + flux_b - next_b)
        if k + 1 < levels:
            above = vertical[k] * (field_ref[k + 1] - here)
            total = total + ((below - above) if k else -above)
            below = above
        else:
            total = total + below
        emit(k, total)


def precondition(resid_ref, inverse_ref, out_ref):
    levels, height, _ = resid_ref.shape
    step = 16
    for block in range(0, levels, BK):
        for at in range(0, height, step):
            rows = slice(at, at + step)
            resid = [resid_ref[block + c, rows, :] for c in range(BK)]
            for k in range(block, block + BK):
                total = inverse_ref[0, k, rows, :].astype(F32) * resid[0]
                for c in range(1, BK):
                    total = total + inverse_ref[c, k, rows, :].astype(F32) * resid[c]
                out_ref[k, rows, :] = total


def by_sublane(values):
    total = values[0:8]
    for at in range(8, values.shape[0], 8):
        total = total + values[at : at + 8]
    return total


def pack_kernel(where_ref, turn_ref, field, metric_a, metric_b, flags, row_up, row_down, col_up, col_down):
    gx, panel = where_ref[0], where_ref[1]
    n_panel, n_gx = turn_ref.shape[1:]
    q = lax.broadcasted_iota(jnp.int32, (n_panel, n_gx), 0)
    g = lax.broadcasted_iota(jnp.int32, (n_panel, n_gx), 1)

    def at(edge, dg, dq):
        gg = lax.rem(gx + dg + n_gx, n_gx)
        qq = lax.rem(panel + dq + n_panel, n_panel)
        picked = jnp.where((g == gg) & (q == qq), turn_ref[edge], 0).astype(F32)
        return jnp.sum(jnp.sum(picked, axis=1, keepdims=True), axis=0, keepdims=True)

    def odd(code):
        return jnp.where((code == 1.0) | (code == 3.0), 1.0, 0.0)

    def sign(code):
        return jnp.where(code >= 2.0, -1.0, 1.0)

    own_a, own_b = at(1, 0, 0), at(3, 0, 0)
    found = (
        odd(at(0, 1, 0)), odd(at(1, -1, 0)), odd(at(2, 0, 1)), odd(at(3, 0, -1)),
        odd(own_a), sign(own_a), odd(own_b), sign(own_b),
    )
    for i, value in enumerate(found):
        flags[i : i + 1, :] = jnp.broadcast_to(value, (1, 128))
    pack(field, flags, row_up, row_down, col_up, col_down, (metric_a, metric_b))


def first_kernel(field, right_side, inverse, *refs):
    coef, halo, (resid, search, *edges), (flux,) = refs[:7], refs[7:15], refs[15:21], refs[21:]

    def emit(k, image):
        resid[k] = right_side[k] - image

    apply_operator(field, coef, halo, flux, emit)
    precondition(resid, inverse, search)
    pack(search, coef[6], *edges)


def second_kernel(field, resid, inverse, *refs):
    coef, halo, (image, search, sums, *edges), (flux,) = refs[:7], refs[7:15], refs[15:22], refs[22:]
    totals = [jnp.zeros((8, 128), F32) for _ in range(2)]

    def emit(k, value):
        image[k] = value
        totals[0] = totals[0] + by_sublane(resid[k] * value)
        totals[1] = totals[1] + by_sublane(value * value)

    apply_operator(field, coef, halo, flux, emit)
    for i, total in enumerate(totals):
        sums[i : i + 1, :] = jnp.sum(total, axis=0, keepdims=True)
    sums[2:, :] = jnp.zeros((6, 128), F32)
    precondition(image, inverse, search)
    pack(search, coef[6], *edges)


def third_kernel(field, resid, first, sums_in, *refs):
    coef, halo, (sums,), (flux,) = refs[:7], refs[7:15], refs[15:16], refs[16:]
    totals = [jnp.zeros((8, 128), F32) for _ in range(3)]

    def emit(k, value):
        totals[0] = totals[0] + by_sublane(first[k] * value)
        totals[1] = totals[1] + by_sublane(value * value)
        totals[2] = totals[2] + by_sublane(resid[k] * value)

    apply_operator(field, coef, halo, flux, emit)
    row = lax.broadcasted_iota(jnp.int32, (8, 128), 0)
    packed = sums_in[...]
    for i, total in enumerate(totals):
        packed = jnp.where(row == 2 + i, jnp.sum(total, axis=0, keepdims=True), packed)
    for i in range(sums.shape[0]):
        sums[i] = packed


def last_kernel(parts, first, second, out):
    total = parts[0]
    for i in range(1, parts.shape[0]):
        total = total + parts[i]
    total = jnp.sum(total, axis=1, keepdims=True)
    cross1, square1, along, square2, cross2 = (total[i : i + 1, :] for i in range(5))
    alpha = cross1 / square1
    ratio = along / square1
    weight2 = (cross2 - ratio * cross1) / (square2 - ratio * along)
    weight1 = alpha - ratio * weight2
    for k in range(first.shape[0]):
        out[k] = weight1 * first[k] + weight2 * second[k]


def call(body, operands, outs, scratch=(), smem=0, flops=1 << 22):
    specs = [pl.BlockSpec(memory_space=pltpu.SMEM)] * smem + [VMEM] * (len(operands) - smem)
    return pl.pallas_call(
        body,
        out_shape=tuple(jax.ShapeDtypeStruct(shape, F32) for shape in outs),
        in_specs=specs,
        out_specs=tuple(VMEM for _ in outs),
        scratch_shapes=tuple(pltpu.VMEM(shape, F32) for shape in scratch),
        compiler_params=pltpu.CompilerParams(vmem_limit_bytes=16 << 20),
        cost_estimate=pl.CostEstimate(flops=flops, bytes_accessed=1 << 20, transcendentals=0),
    )(*operands)


def shift(block, axis, distance):
    count = lax.axis_size(axis)
    return lax.ppermute(block, axis, [((i - distance) % count, i) for i in range(count)])


def exchange(row_up, row_down, col_up, col_down):
    low_row = shift(row_up, GX, 1)
    low_col = shift(col_up, PANEL, 1)
    high_row = shift(row_down, GX, -1)
    high_col = shift(col_down, PANEL, -1)
    return low_row, high_row, low_col, high_col


def sum_over(parts, axes):
    return lax.all_to_all(parts, axes, 0, 0, tiled=True)


def shards(
    right_side, previous, diagonal, vertical, metric_a, metric_b, profile, column_inverse, edge_turn
):
    levels, height, width = right_side.shape
    place = jnp.stack([lax.axis_index(GX), lax.axis_index(PANEL)]).astype(jnp.int32)
    spread = jnp.broadcast_to(jnp.pad(profile, (0, ROWS - levels))[:, None], (ROWS, width))
    lanes = jnp.broadcast_to(jnp.pad(profile, (0, width - levels))[None], (8, width))
    row, col, field, sums = (ROWS, width), (height, width), right_side.shape, (8, width)
    edges = [row, row, col, col]

    flags, *sent = call(
        pack_kernel,
        (place, jnp.transpose(edge_turn, (0, 2, 1)), previous, metric_a, metric_b),
        [(8, width), *edges],
        smem=1,
    )
    coef = (diagonal, vertical, metric_a, metric_b, spread, lanes, flags)
    halo = exchange(*sent)
    metrics = (halo[1], halo[3])
    resid, search_first, *sent1 = call(
        first_kernel,
        (previous, right_side, column_inverse, *coef, *halo, sent[0], sent[2], *metrics),
        [field, field, *edges],
        [row],
    )
    halo = exchange(*sent1)
    image_first, search_next, part, *sent2 = call(
        second_kernel,
        (search_first, resid, column_inverse, *coef, *halo, sent1[0], sent1[2], *metrics),
        [field, field, sums, *edges],
        [row],
    )
    halo = exchange(*sent2)
    plane = lax.axis_size(PLANE)
    depth = lax.axis_size(COLUMN)
    (parts,) = call(
        third_kernel,
        (search_next, resid, image_first, part, *coef, *halo, sent2[0], sent2[2], *metrics),
        [(plane, *sums)],
        [row],
    )
    part = jnp.sum(sum_over(parts, PLANE), axis=0)
    parts = sum_over(jnp.broadcast_to(part[None], (depth, *sums)), COLUMN)
    (increment,) = call(last_kernel, (parts, search_first, search_next), [field])
    return increment


def solution(mesh):
    finer = Mesh(
        mesh.devices.reshape(SHAPE), ("panel_0", "panel_1", "gx_0", "gx_1", "gx_2")
    )
    spec = P(None, GX, PANEL)
    in_specs = (
        spec, spec, spec, spec, P(GX, PANEL), P(GX, PANEL), P(), P(None, None, GX, PANEL), P(),
    )
    return jax.shard_map(shards, mesh=finer, in_specs=in_specs, out_specs=spec, check_vma=False)
```

time: 242 us -> 116 us (0.48)
  blocking collectives: 108 us -> 35.3 us
  other arithmetic: 26.9 us -> 0.11 us
  local copies, waits for them, and re-layouts: 32 us -> 11.9 us
  between operations: 14.7 us -> 0.19 us
  Pallas kernels: 0 us -> 8.14 us
  waiting for transfers between devices: 5.07 us -> 9.02 us
  starting transfers between devices: 53.9 us -> 50.8 us
    psum x10 -> x0, blocking collectives: 108 us -> none  [by_axis(): return functools.reduce(lax.psum, axes, shard)]
    all_to_all x0 -> x2, blocking collectives: none -> 35.3 us  [sum_over(): return lax.all_to_all(parts, axes, 0, 0, tiled=True)]
    slice x19 -> x0, local copies, waits for them, and re-layouts: 16.6 us -> none  [the longest x3 3.93 us: assemble(): next_a = jnp.concatenate([flux_a[:, 1:], high_a[:, None]], axis=1)]
    mul x6 -> x0, other arithmetic: 10.4 us -> none  [the longest x3 6.3 us: local_fluxes(): return (face_a * (pressure - prev_a), face_b * (pressure - prev_b))]
    reduce_sum x2 -> x1, other arithmetic: 8.18 us -> 0.04 us  [shards(): part = jnp.sum(sum_over(parts, PLANE), axis=0)]
    pallas_call x0 -> x5, Pallas kernels: none -> 8.14 us  [call(): pl.pallas_call(body, out_shape=tuple((jax.ShapeDtypeStruct(shape, F32) fo...]
    broadcast_in_dim x6 -> x3, local copies, waits for them, and re-layouts: 7.41 us -> 0.08 us  [the longest x1 0.07 us: shards(): jnp.broadcast_to(jnp.pad(profile, (0, ROWS - levels))[:, None], (ROWS, wi...]
    unnamed x34 -> x28, local copies, waits for them, and re-layouts: 3.28 us -> 10.5 us
  transfers between devices with their start and end apart: 12 -> 12, of which waited for: 2 -> 3; matrix products, arithmetic and copies ran while one was open for 10% -> 1% of each run, Pallas kernels for 0% -> 0%
where the time goes in v1:
time: 116 us; the launch traced here: 115 us
  starting transfers between devices  50.8 us (44%)
  blocking collectives  35.3 us (30%)
  local copies, waits for them, and re-layouts  11.9 us (10%)
  waiting for transfers between devices  9.02 us (8%)
  Pallas kernels  8.14 us (7%)
    ppermute x12, starting transfers between devices, shift(): lax.ppermute(block, axis, [((i - distance) % count, i) for i in range(cou...  50.8 us
    all_to_all x2, blocking collectives, sum_over(): return lax.all_to_all(parts, axes, 0, 0, tiled=True)  35.3 us
    unnamed x28, local copies, waits for them, and re-layouts  10.5 us
    ppermute x12, waiting for transfers between devices, shift(): lax.ppermute(block, axis, [((i - distance) % count, i) for i in range(cou...  9.02 us
    pallas_call x5, Pallas kernels, call(): pl.pallas_call(body, out_shape=tuple((jax.ShapeDtypeStruct(shape, F32) fo...  8.14 us
  transfers between devices with their start and end apart: 12, of which 3 were waited for; matrix products, arithmetic and copies ran while one was open for 1% of the time, Pallas kernels for 0%

profile of v1, /device:TPU:1, one launch (start us, length us, event | category | flops | bytes accessed | tf_op | source)
XLA Modules:
  0.0 115.4 jit_solution(8508765376284554116)
XLA Ops:
  0.1 1.1 copy-done.6
  4.4 6.4 %collective-permute-start.3 = (f32[64,128]{1,0:T(8,128)S(1)}, f32[64,128]{1,0:T(8,128)S(1)}, u32[]{:S(2)}, u32[]{:S(2)}) collective-permute-start(f32[64,128]{1,0:T(8,128)S(1)} %get-tuple-element.27), channel_id=1, source_target_pairs={{64,0},{128,64},{192,128},{256,192},{320,256},{384,320},{448,384},... | collective-permute-start | bytes 98312 | tf_op jit(solution)/shard_map/ppermute | solution.py:235
  10.8 1.9 %collective-permute-start.2 = (f32[64,128]{1,0:T(8,128)S(1)}, f32[64,128]{1,0:T(8,128)S(1)}, u32[]{:S(2)}, u32[]{:S(2)}) collective-permute-start(f32[64,128]{1,0:T(8,128)S(1)} %get-tuple-element.26.refs_12_), channel_id=1, source_target_pairs={{448,0},{0,64},{64,128},{128,192},{192,256},{256,320},{320,384},{3... | collective-permute-start | bytes 98312 | tf_op jit(solution)/shard_map/ppermute | solution.py:235
  12.7 6.3 %collective-permute-start.1 = (f32[24,128]{1,0:T(8,128)S(1)}, f32[24,128]{1,0:T(8,128)S(1)}, u32[]{:S(2)}, u32[]{:S(2)}) collective-permute-start(f32[24,128]{1,0:T(8,128)S(1)} %get-tuple-element.25), channel_id=1, source_target_pairs={{1,0},{2,1},{3,2},{4,3},{5,4},{6,5},{7,6},{8,7},{9,8},{10,9},{11,1... | collective-permute-start | bytes 36872 | tf_op jit(solution)/shard_map/ppermute | solution.py:235
  19.0 1.9 %collective-permute-start = (f32[24,128]{1,0:T(8,128)S(1)}, f32[24,128]{1,0:T(8,128)S(1)}, u32[]{:S(2)}, u32[]{:S(2)}) collective-permute-start(f32[24,128]{1,0:T(8,128)S(1)} %get-tuple-element.24.refs_11_), channel_id=1, source_target_pairs={{63,0},{0,1},{1,2},{2,3},{3,4},{4,5},{5,6},{6,7},{7,8},{8,9},{9,10... | collective-permute-start | bytes 36872 | tf_op jit(solution)/shard_map/ppermute | solution.py:235
  22.3 6.7 %collective-permute-done.refs_7_ = f32[24,128]{1,0:T(8,128)S(1)} collective-permute-done((f32[24,128]{1,0:T(8,128)S(1)}, f32[24,128]{1,0:T(8,128)S(1)}, u32[]{:S(2)}, u32[]{:S(2)}) %collective-permute-start) | collective-permute-done | bytes 12320 | tf_op jit(solution)/shard_map/ppermute | solution.py:235
  29.1 1.1 copy-done
  31.2 1.3 %copy-done.4 = bf16[4,20,64,128]{3,2,1,0:T(8,128)(2,1)S(1)} copy-done((bf16[4,20,64,128]{3,2,1,0:T(8,128)(2,1)S(1)}, bf16[4,20,64,128]{3,2,1,0:T(8,128)(2,1)}, u32[]{:S(2)}) %copy-start.4) | copy-done | bytes 1310744
  32.5 1.1 copy-done.7
  36.2 2.2 %shard_map.92 = (f32[20,64,128]{2,1,0:T(8,128)S(1)}, f32[20,64,128]{2,1,0:T(8,128)S(1)}, f32[24,128]{1,0:T(8,128)S(1)}, f32[24,128]{1,0:T(8,128)S(1)}, f32[64,128]{1,0:T(8,128)S(1)}, /*index=5*/f32[64,128]{1,0:T(8,128)S(1)}) custom-call(f32[20,64,128]{2,1,0:T(8,128)S(1)} %copy-done.7, f32[20,64,128]{2,1,0:T(8,128)S(1)} %copy-done.8, ...), custom_call_target="tpu_custom_call" | custom-call | flops 4194304 | bytes 1048576 | tf_op jit(solution)/shard_map/pallas_call | solution.py:222
  38.5 4.9 %collective-permute-start.7 = (f32[64,128]{1,0:T(8,128)S(1)}, f32[64,128]{1,0:T(8,128)S(1)}, u32[]{:S(2)}, u32[]{:S(2)}) collective-permute-start(f32[64,128]{1,0:T(8,128)S(1)} %get-tuple-element.33), channel_id=1, source_target_pairs={{64,0},{128,64},{192,128},{256,192},{320,256},{384,320},{448,384},... | collective-permute-start | bytes 98312 | tf_op jit(solution)/shard_map/ppermute | solution.py:235
  43.3 1.9 %collective-permute-start.6 = (f32[64,128]{1,0:T(8,128)S(1)}, f32[64,128]{1,0:T(8,128)S(1)}, u32[]{:S(2)}, u32[]{:S(2)}) collective-permute-start(f32[64,128]{1,0:T(8,128)S(1)} %get-tuple-element.32.refs_12_), channel_id=1, source_target_pairs={{448,0},{0,64},{64,128},{128,192},{192,256},{256,320},{320,384},{3... | collective-permute-start | bytes 98312 | tf_op jit(solution)/shard_map/ppermute | solution.py:235
  45.3 8.2 %collective-permute-start.5 = (f32[24,128]{1,0:T(8,128)S(1)}, f32[24,128]{1,0:T(8,128)S(1)}, u32[]{:S(2)}, u32[]{:S(2)}) collective-permute-start(f32[24,128]{1,0:T(8,128)S(1)} %get-tuple-element.31), channel_id=1, source_target_pairs={{1,0},{2,1},{3,2},{4,3},{5,4},{6,5},{7,6},{8,7},{9,8},{10,9},{11,1... | collective-permute-start | bytes 36872 | tf_op jit(solution)/shard_map/ppermute | solution.py:235
  53.5 1.9 %collective-permute-start.4 = (f32[24,128]{1,0:T(8,128)S(1)}, f32[24,128]{1,0:T(8,128)S(1)}, u32[]{:S(2)}, u32[]{:S(2)}) collective-permute-start(f32[24,128]{1,0:T(8,128)S(1)} %get-tuple-element.30.refs_11_), channel_id=1, source_target_pairs={{63,0},{0,1},{1,2},{2,3},{3,4},{4,5},{5,6},{6,7},{7,8},{8,9},{9,10... | collective-permute-start | bytes 36872 | tf_op jit(solution)/shard_map/ppermute | solution.py:235
  55.5 1.1 collective-permute-done.4.refs_7_
  56.6 2.2 %shard_map.93 = (f32[20,64,128]{2,1,0:T(8,128)S(1)}, f32[20,64,128]{2,1,0:T(8,128)S(1)}, f32[8,128]{1,0:T(8,128)S(1)}, f32[24,128]{1,0:T(8,128)S(1)}, f32[24,128...) custom-call(f32[20,64,128]{2,1,0:T(8,128)S(1)} %get-tuple-element.28.field.first, ...), custom_call_target="tpu_custom_call" | custom-call | flops 4194304 | bytes 1048576 | tf_op jit(solution)/shard_map/pallas_call | solution.py:222
  58.9 5.8 %collective-permute-start.11 = (f32[64,128]{1,0:T(8,128)S(1)}, f32[64,128]{1,0:T(8,128)S(1)}, u32[]{:S(2)}, u32[]{:S(2)}) collective-permute-start(f32[64,128]{1,0:T(8,128)S(1)} %get-tuple-element.40), channel_id=1, source_target_pairs={{64,0},{128,64},{192,128},{256,192},{320,256},{384,320},{448,384},... | collective-permute-start | bytes 98312 | tf_op jit(solution)/shard_map/ppermute | solution.py:235
  64.6 1.9 %collective-permute-start.10 = (f32[64,128]{1,0:T(8,128)S(1)}, f32[64,128]{1,0:T(8,128)S(1)}, u32[]{:S(2)}, u32[]{:S(2)}) collective-permute-start(f32[64,128]{1,0:T(8,128)S(1)} %get-tuple-element.39.refs_12_), channel_id=1, source_target_pairs={{448,0},{0,64},{64,128},{128,192},{192,256},{256,320},{320,384},{3... | collective-permute-start | bytes 98312 | tf_op jit(solution)/shard_map/ppermute | solution.py:235
  66.5 7.8 %collective-permute-start.9 = (f32[24,128]{1,0:T(8,128)S(1)}, f32[24,128]{1,0:T(8,128)S(1)}, u32[]{:S(2)}, u32[]{:S(2)}) collective-permute-start(f32[24,128]{1,0:T(8,128)S(1)} %get-tuple-element.38), channel_id=1, source_target_pairs={{1,0},{2,1},{3,2},{4,3},{5,4},{6,5},{7,6},{8,7},{9,8},{10,9},{11,1... | collective-permute-start | bytes 36872 | tf_op jit(solution)/shard_map/ppermute | solution.py:235
  74.3 1.9 %collective-permute-start.8 = (f32[24,128]{1,0:T(8,128)S(1)}, f32[24,128]{1,0:T(8,128)S(1)}, u32[]{:S(2)}, u32[]{:S(2)}) collective-permute-start(f32[24,128]{1,0:T(8,128)S(1)} %get-tuple-element.37.refs_11_), channel_id=1, source_target_pairs={{63,0},{0,1},{1,2},{2,3},{3,4},{4,5},{5,6},{6,7},{7,8},{8,9},{9,10... | collective-permute-start | bytes 36872 | tf_op jit(solution)/shard_map/ppermute | solution.py:235
  76.2 1.1 collective-permute-done.8.refs_7_
  77.4 1.7 %shard_map.94 = f32[32,8,128]{2,1,0:T(8,128)S(1)} custom-call(f32[20,64,128]{2,1,0:T(8,128)S(1)} %get-tuple-element.34.field.second, f32[20,64,128]{2,1,0:T(8,128)S(1)} %get-tuple-element.29.resid, f32[20,64,128]{2,1,0:T(8,128)S(1)} %get-tuple-element.35.first, f32[8,128]{1,0:T(8,128)S(1)} %get-tuple-element.36.sums_in, f32[20,64,128]{2,1,0:T(8,128)S(1)} %copy-done.1, ...), custom_call_target="tpu_custom_call" | custom-call | flops 4194304 | bytes 1048576 | tf_op jit(solution)/shard_map/pallas_call | solution.py:222
  79.0 18.4 %all_to_all.10 = f32[32,8,128]{2,1,0:T(8,128)S(1)} all-to-all(f32[32,8,128]{2,1,0:T(8,128)S(1)} %shard_map.94), channel_id=1, replica_groups=mesh['panel_0'=2,'panel_1'=4,'gx_0'=16,'gx_1'=2,'gx_2'=2] {'panel_0','pa..., dimensions={0} | all-to-all | bytes 262144 | tf_op jit(solution)/shard_map/all_to_all | solution.py:247
  97.5 16.9 %all_to_all.11.parts = f32[16,8,128]{2,1,0:T(8,128)S(1)} all-to-all(f32[16,8,128]{2,1,0:T(8,128)S(1)} %broadcast_in_dim.8), channel_id=1, replica_groups=mesh['panel_0'=2,'panel_1'=4,'gx_0'=16,'gx_1'=2,'gx_2'=2] {'gx_0'}, dimensions={0} | all-to-all | bytes 131072 | tf_op jit(solution)/shard_map/all_to_all | solution.py:247
  (42 shorter events, 9.5 us)
Async XLA Ops:
  0.1 1.1 copy-start.6
  1.9 0.8 copy-start.11
  4.4 24.6 %collective-permute-start.3 = (f32[64,128]{1,0:T(8,128)S(1)}, f32[64,128]{1,0:T(8,128)S(1)}, u32[]{:S(2)}, u32[]{:S(2)}) collective-permute-start(f32[64,128]{1,0:T(8,128)S(1)} %get-tuple-element.27), channel_id=1, source_target_pairs={{64,0},{128,64},{192,128},{256,192},{320,256},{384,320},{448,384},... | collective-permute-start | bytes 98312 | tf_op jit(solution)/shard_map/ppermute | solution.py:235
  10.8 18.2 %collective-permute-start.2 = (f32[64,128]{1,0:T(8,128)S(1)}, f32[64,128]{1,0:T(8,128)S(1)}, u32[]{:S(2)}, u32[]{:S(2)}) collective-permute-start(f32[64,128]{1,0:T(8,128)S(1)} %get-tuple-element.26.refs_12_), channel_id=1, source_target_pairs={{448,0},{0,64},{64,128},{128,192},{192,256},{256,320},{320,384},{3... | collective-permute-start | bytes 98312 | tf_op jit(solution)/shard_map/ppermute | solution.py:235
  12.7 9.5 %collective-permute-start.1 = (f32[24,128]{1,0:T(8,128)S(1)}, f32[24,128]{1,0:T(8,128)S(1)}, u32[]{:S(2)}, u32[]{:S(2)}) collective-permute-start(f32[24,128]{1,0:T(8,128)S(1)} %get-tuple-element.25), channel_id=1, source_target_pairs={{1,0},{2,1},{3,2},{4,3},{5,4},{6,5},{7,6},{8,7},{9,8},{10,9},{11,1... | collective-permute-start | bytes 36872 | tf_op jit(solution)/shard_map/ppermute | solution.py:235
  19.0 10.0 %collective-permute-start = (f32[24,128]{1,0:T(8,128)S(1)}, f32[24,128]{1,0:T(8,128)S(1)}, u32[]{:S(2)}, u32[]{:S(2)}) collective-permute-start(f32[24,128]{1,0:T(8,128)S(1)} %get-tuple-element.24.refs_11_), channel_id=1, source_target_pairs={{63,0},{0,1},{1,2},{2,3},{3,4},{4,5},{5,6},{6,7},{7,8},{8,9},{9,10... | collective-permute-start | bytes 36872 | tf_op jit(solution)/shard_map/ppermute | solution.py:235
  29.1 1.1 copy-start
  30.2 1.1 copy-start.2
  31.2 1.3 %copy-start.4 = (bf16[4,20,64,128]{3,2,1,0:T(8,128)(2,1)S(1)}, bf16[4,20,64,128]{3,2,1,0:T(8,128)(2,1)}, u32[]{:S(2)}) copy-start(bf16[4,20,64,128]{3,2,1,0:T(8,128)(2,1)} %inverse.3) | copy-start | bytes 3932164
  32.5 1.1 copy-start.7
  33.6 1.1 copy-start.8
  34.7 0.8 copy-start.10
  35.5 0.8 copy-start.12
  36.2 20.4 %copy-start.1 = (f32[20,64,128]{2,1,0:T(8,128)S(1)}, f32[20,64,128]{2,1,0:T(8,128)}, u32[]{:S(2)}) copy-start(f32[20,64,128]{2,1,0:T(8,128)} %refs_0_.5) | copy-start | bytes 1966084
  36.2 20.4 %copy-start.3 = (f32[19,64,128]{2,1,0:T(8,128)S(1)}, f32[19,64,128]{2,1,0:T(8,128)}, u32[]{:S(2)}) copy-start(f32[19,64,128]{2,1,0:T(8,128)} %refs_1_.5) | copy-start | bytes 1867780
  36.2 20.4 %copy-start.5 = (bf16[4,20,64,128]{3,2,1,0:T(8,128)(2,1)S(1)}, bf16[4,20,64,128]{3,2,1,0:T(8,128)(2,1)}, u32[]{:S(2)}) copy-start(bf16[4,20,64,128]{3,2,1,0:T(8,128)(2,1)} %inverse.3) | copy-start | bytes 3932164
  38.5 18.1 %collective-permute-start.7 = (f32[64,128]{1,0:T(8,128)S(1)}, f32[64,128]{1,0:T(8,128)S(1)}, u32[]{:S(2)}, u32[]{:S(2)}) collective-permute-start(f32[64,128]{1,0:T(8,128)S(1)} %get-tuple-element.33), channel_id=1, source_target_pairs={{64,0},{128,64},{192,128},{256,192},{320,256},{384,320},{448,384},... | collective-permute-start | bytes 98312 | tf_op jit(solution)/shard_map/ppermute | solution.py:235
  43.3 13.3 %collective-permute-start.6 = (f32[64,128]{1,0:T(8,128)S(1)}, f32[64,128]{1,0:T(8,128)S(1)}, u32[]{:S(2)}, u32[]{:S(2)}) collective-permute-start(f32[64,128]{1,0:T(8,128)S(1)} %get-tuple-element.32.refs_12_), channel_id=1, source_target_pairs={{448,0},{0,64},{64,128},{128,192},{192,256},{256,320},{320,384},{3... | collective-permute-start | bytes 98312 | tf_op jit(solution)/shard_map/ppermute | solution.py:235
  45.3 10.2 %collective-permute-start.5 = (f32[24,128]{1,0:T(8,128)S(1)}, f32[24,128]{1,0:T(8,128)S(1)}, u32[]{:S(2)}, u32[]{:S(2)}) collective-permute-start(f32[24,128]{1,0:T(8,128)S(1)} %get-tuple-element.31), channel_id=1, source_target_pairs={{1,0},{2,1},{3,2},{4,3},{5,4},{6,5},{7,6},{8,7},{9,8},{10,9},{11,1... | collective-permute-start | bytes 36872 | tf_op jit(solution)/shard_map/ppermute | solution.py:235
  53.5 3.1 %collective-permute-start.4 = (f32[24,128]{1,0:T(8,128)S(1)}, f32[24,128]{1,0:T(8,128)S(1)}, u32[]{:S(2)}, u32[]{:S(2)}) collective-permute-start(f32[24,128]{1,0:T(8,128)S(1)} %get-tuple-element.30.refs_11_), channel_id=1, source_target_pairs={{63,0},{0,1},{1,2},{2,3},{3,4},{4,5},{5,6},{6,7},{7,8},{8,9},{9,10... | collective-permute-start | bytes 36872 | tf_op jit(solution)/shard_map/ppermute | solution.py:235
  58.9 18.5 %collective-permute-start.11 = (f32[64,128]{1,0:T(8,128)S(1)}, f32[64,128]{1,0:T(8,128)S(1)}, u32[]{:S(2)}, u32[]{:S(2)}) collective-permute-start(f32[64,128]{1,0:T(8,128)S(1)} %get-tuple-element.40), channel_id=1, source_target_pairs={{64,0},{128,64},{192,128},{256,192},{320,256},{384,320},{448,384},... | collective-permute-start | bytes 98312 | tf_op jit(solution)/shard_map/ppermute | solution.py:235
  64.6 12.8 %collective-permute-start.10 = (f32[64,128]{1,0:T(8,128)S(1)}, f32[64,128]{1,0:T(8,128)S(1)}, u32[]{:S(2)}, u32[]{:S(2)}) collective-permute-start(f32[64,128]{1,0:T(8,128)S(1)} %get-tuple-element.39.refs_12_), channel_id=1, source_target_pairs={{448,0},{0,64},{64,128},{128,192},{192,256},{256,320},{320,384},{3... | collective-permute-start | bytes 98312 | tf_op jit(solution)/shard_map/ppermute | solution.py:235
  66.5 9.7 %collective-permute-start.9 = (f32[24,128]{1,0:T(8,128)S(1)}, f32[24,128]{1,0:T(8,128)S(1)}, u32[]{:S(2)}, u32[]{:S(2)}) collective-permute-start(f32[24,128]{1,0:T(8,128)S(1)} %get-tuple-element.38), channel_id=1, source_target_pairs={{1,0},{2,1},{3,2},{4,3},{5,4},{6,5},{7,6},{8,7},{9,8},{10,9},{11,1... | collective-permute-start | bytes 36872 | tf_op jit(solution)/shard_map/ppermute | solution.py:235
  74.3 3.1 %collective-permute-start.8 = (f32[24,128]{1,0:T(8,128)S(1)}, f32[24,128]{1,0:T(8,128)S(1)}, u32[]{:S(2)}, u32[]{:S(2)}) collective-permute-start(f32[24,128]{1,0:T(8,128)S(1)} %get-tuple-element.37.refs_11_), channel_id=1, source_target_pairs={{63,0},{0,1},{1,2},{2,3},{3,4},{4,5},{5,6},{6,7},{7,8},{8,9},{9,10... | collective-permute-start | bytes 36872 | tf_op jit(solution)/shard_map/ppermute | solution.py:235
  (2 other events, 1.5 us)

commit v2 on v1

v2 whole, which is shorter than its diff:
```python
import jax
import jax.numpy as jnp
from jax import lax
from jax.experimental import pallas as pl
from jax.experimental.pallas import tpu as pltpu
from jax.sharding import Mesh
from jax.sharding import PartitionSpec as P

BK = 4
SHAPE = (2, 4, 16, 2, 2)
GX = ("gx_0", "gx_1", "gx_2")
PANEL = ("panel_0", "panel_1")
PLANE = ("panel_0", "panel_1", "gx_1", "gx_2")
COLUMN = ("gx_0",)
ROWS = 24
LOAD_LIMIT = 16 << 20
METRIC = 20
F32 = jnp.float32
VMEM = pl.BlockSpec(memory_space=pltpu.VMEM)
HBM = pl.BlockSpec(memory_space=pltpu.HBM)


def reverse_lanes(values, length):
    lane = lax.broadcasted_iota(jnp.int32, values.shape, 1)
    index = jnp.where(lane < length, length - 1 - lane, lane)
    return jnp.take_along_axis(values, index, axis=1)


def reverse_rows(values):
    count = values.shape[0] // 8
    row = lax.broadcasted_iota(jnp.int32, (8, 128), 0)
    parts = [
        jnp.take_along_axis(values[8 * i : 8 * i + 8], 7 - row, axis=0)
        for i in reversed(range(count))
    ]
    return jnp.concatenate(parts, axis=0)


def flag(flags_ref, at):
    return flags_ref[at : at + 1, :]


def pack(field_ref, flags_ref, row_ref, edges, metrics=None):
    up_ref, down_ref = row_ref
    row_near, row_far, col_near, col_far = edges
    levels, height, width = field_ref.shape
    lane = lax.broadcasted_iota(jnp.int32, (height, width), 1)
    for k in range(levels):
        up_ref[k : k + 1, :] = field_ref[k, height - 1 : height, :]
        down_ref[k : k + 1, :] = field_ref[k, 0:1, :]
    for k in range(levels, ROWS):
        up_ref[k : k + 1, :] = jnp.zeros((1, width), F32)
        down_ref[k : k + 1, :] = jnp.zeros((1, width), F32)
    last = jnp.zeros((height, width), F32)
    first = jnp.zeros((height, width), F32)
    for k in range(levels):
        values = field_ref[k]
        last = jnp.where(lane == k, pltpu.roll(values, (k + 1) % width, 1), last)
        first = jnp.where(lane == k, pltpu.roll(values, k, 1) if k else values, first)
    if metrics is not None:
        metric_a, metric_b = metrics
        down_ref[METRIC : METRIC + 1, :] = metric_a[0:1, :]
        first = jnp.where(lane == METRIC, pltpu.roll(metric_b[...], METRIC, 1), first)
    up, down = up_ref[...], down_ref[...]
    up = jnp.where(flag(flags_ref, 0) > 0.5, reverse_lanes(up, width), up)
    down = jnp.where(flag(flags_ref, 1) > 0.5, reverse_lanes(down, width), down)
    last = jnp.where(flag(flags_ref, 2) > 0.5, reverse_rows(last), last)
    first = jnp.where(flag(flags_ref, 3) > 0.5, reverse_rows(first), first)
    even_a, even_b = flag(flags_ref, 8) > 0.5, flag(flags_ref, 9) > 0.5
    row_near[...] = jnp.where(even_a, up, down)
    row_far[...] = jnp.where(even_a, down, up)
    col_near[...] = jnp.where(even_b, last, first)
    col_far[...] = jnp.where(even_b, first, last)


def neighbours(flags_ref, got, sent):
    even_a, even_b = flag(flags_ref, 8) > 0.5, flag(flags_ref, 9) > 0.5
    row_near, row_far, col_near, col_far = (ref[...] for ref in got)
    own_near, own_far, mine_near, mine_far = (ref[...] for ref in sent)
    return (
        jnp.where(even_a, row_far, row_near), jnp.where(even_a, row_near, row_far),
        jnp.where(even_b, col_far, col_near), jnp.where(even_b, col_near, col_far),
        jnp.where(even_a, own_near, own_far), jnp.where(even_b, mine_near, mine_far),
    )


def apply_operator(field_ref, coef, near, faces, scratch, emit):
    diagonal, vertical, metric_a, metric_b, spread, _, flags_ref = coef
    low, high_row, low_col, high_col, own_row, own_col = near
    face_row, face_col = faces
    low_row, flux_ref = scratch
    levels, height, width = field_ref.shape
    row = lax.broadcasted_iota(jnp.int32, (height, width), 0)
    lane = lax.broadcasted_iota(jnp.int32, (height, width), 1)
    low_row[...] = low
    own_row = jnp.where(flag(flags_ref, 4) > 0.5, reverse_lanes(own_row, width), own_row)
    flux_ref[...] = flag(flags_ref, 5) * (face_row * (high_row - own_row))
    own_col = jnp.where(flag(flags_ref, 6) > 0.5, reverse_rows(own_col), own_col)
    flux_col = flag(flags_ref, 7) * (face_col * (high_col - own_col))
    below = None
    for k in range(levels):
        here = field_ref[k]
        scale = spread[k : k + 1, :]
        face_a = metric_a[...] * scale
        face_b = metric_b[...] * scale
        prev_a = jnp.where(row == 0, low_row[k : k + 1, :], pltpu.roll(here, 1, 0))
        edge = pltpu.roll(low_col, width - k, 1) if k else low_col
        prev_b = jnp.where(lane == 0, edge, pltpu.roll(here, 1, 1))
        flux_a = face_a * (here - prev_a)
        flux_b = face_b * (here - prev_b)
        next_a = jnp.where(
            row == height - 1, flux_ref[k : k + 1, :], pltpu.roll(flux_a, height - 1, 0)
        )
        next_b = jnp.where(
            lane == width - 1,
            pltpu.roll(flux_col, width - 1 - k, 1),
            pltpu.roll(flux_b, width - 1, 1),
        )
        total = diagonal[k] * here + (flux_a - next_a + flux_b - next_b)
        if k + 1 < levels:
            above = vertical[k] * (field_ref[k + 1] - here)
            total = total + ((below - above) if k else -above)
            below = above
        else:
            total = total + below
        emit(k, total)


def precondition(resid_ref, inverse_ref, out_ref):
    levels, height, _ = resid_ref.shape
    step = 16
    for block in range(0, levels, BK):
        for at in range(0, height, step):
            rows = slice(at, at + step)
            resid = [resid_ref[block + c, rows, :] for c in range(BK)]
            for k in range(block, block + BK):
                total = inverse_ref[0, k, rows, :].astype(F32) * resid[0]
                for c in range(1, BK):
                    total = total + inverse_ref[c, k, rows, :].astype(F32) * resid[c]
                out_ref[k, rows, :] = total


def by_sublane(values):
    total = values[0:8]
    for at in range(8, values.shape[0], 8):
        total = total + values[at : at + 8]
    return total


def load_kernel(turn, profile, *refs):
    sources, outs, scratch = refs[:7], refs[7:21], refs[21:]
    copies_to, (spread, lanes, flags), edges = outs[:7], outs[7:10], outs[10:]
    turn_ref, profile_ref, up_ref, down_ref, sems = scratch
    pairs = [(turn, turn_ref), (profile, profile_ref), *zip(sources, copies_to)]
    copies = [pltpu.make_async_copy(a, b, sems.at[i]) for i, (a, b) in enumerate(pairs)]
    for copy in copies:
        copy.start()
    gx, panel = lax.axis_index(GX), lax.axis_index(PANEL)
    n_panel, n_gx = turn.shape[1:]
    q = lax.broadcasted_iota(jnp.int32, (n_panel, n_gx), 0)
    g = lax.broadcasted_iota(jnp.int32, (n_panel, n_gx), 1)
    copies[0].wait()

    def at(edge, dg, dq):
        gg = lax.rem(gx + dg + n_gx, n_gx)
        qq = lax.rem(panel + dq + n_panel, n_panel)
        picked = jnp.where((g == gg) & (q == qq), turn_ref[edge], 0).astype(F32)
        return jnp.sum(jnp.sum(picked, axis=1, keepdims=True), axis=0, keepdims=True)

    def odd(code):
        return jnp.where((code == 1.0) | (code == 3.0), 1.0, 0.0)

    def sign(code):
        return jnp.where(code >= 2.0, -1.0, 1.0)

    def even(place):
        return jnp.full((1, 128), 1 - lax.rem(place, 2), jnp.int32).astype(F32)

    own_a, own_b = at(1, 0, 0), at(3, 0, 0)
    found = (
        odd(at(0, 1, 0)), odd(at(1, -1, 0)), odd(at(2, 0, 1)), odd(at(3, 0, -1)),
        odd(own_a), sign(own_a), odd(own_b), sign(own_b), even(gx), even(panel),
    )
    for i, value in enumerate(found):
        flags[i : i + 1, :] = jnp.broadcast_to(value, (1, 128))
    copies[1].wait()
    levels = sources[0].shape[0]
    lane = lax.broadcasted_iota(jnp.int32, lanes.shape, 1)
    in_lanes = jnp.zeros(lanes.shape, F32)
    for k in range(levels):
        spread[k : k + 1, :] = jnp.full((1, spread.shape[1]), profile_ref[k], F32)
        in_lanes = jnp.where(lane == k, profile_ref[k], in_lanes)
    spread[levels:, :] = jnp.zeros((ROWS - levels, spread.shape[1]), F32)
    lanes[...] = in_lanes
    for copy in copies[2:5]:
        copy.wait()
    pack(copies_to[0], flags, (up_ref, down_ref), edges, copies_to[1:3])
    for copy in copies[5:]:
        copy.wait()


def first_kernel(field, right_side, inverse, *refs):
    coef, got, sent, outs, scratch = refs[:7], refs[7:11], refs[11:15], refs[15:23], refs[23:]
    (resid, search, face_row, face_col), edges = outs[:4], outs[4:]
    near = neighbours(coef[6], got, sent)
    face_row[...] = near[1][METRIC : METRIC + 1, :] * coef[4][...]
    face_col[...] = near[3][:, METRIC : METRIC + 1] * coef[5][0:1, :]

    def emit(k, image):
        resid[k] = right_side[k] - image

    apply_operator(field, coef, near, (face_row[...], face_col[...]), scratch, emit)
    precondition(resid, inverse, search)
    pack(search, coef[6], scratch, edges)


def second_kernel(field, resid, inverse, face_row, face_col, *refs):
    coef, got, sent, outs, scratch = refs[:7], refs[7:11], refs[11:15], refs[15:22], refs[22:]
    (image, search, sums), edges = outs[:3], outs[3:]
    totals = [jnp.zeros((8, 128), F32) for _ in range(2)]

    def emit(k, value):
        image[k] = value
        totals[0] = totals[0] + by_sublane(resid[k] * value)
        totals[1] = totals[1] + by_sublane(value * value)

    near = neighbours(coef[6], got, sent)
    apply_operator(field, coef, near, (face_row[...], face_col[...]), scratch, emit)
    for i, total in enumerate(totals):
        sums[i] = total
    precondition(image, inverse, search)
    pack(search, coef[6], scratch, edges)


def third_kernel(field, resid, first, sums, face_row, face_col, *refs):
    coef, got, sent, (out,), scratch = refs[:7], refs[7:11], refs[11:15], refs[15:16], refs[16:]
    totals = [jnp.zeros((8, 128), F32) for _ in range(3)]

    def emit(k, value):
        totals[0] = totals[0] + by_sublane(first[k] * value)
        totals[1] = totals[1] + by_sublane(value * value)
        totals[2] = totals[2] + by_sublane(resid[k] * value)

    near = neighbours(coef[6], got, sent)
    apply_operator(field, coef, near, (face_row[...], face_col[...]), scratch, emit)
    row = lax.broadcasted_iota(jnp.int32, (8, 128), 0)
    lane = lax.broadcasted_iota(jnp.int32, (8, 128), 1)
    packed = jnp.zeros((8, 128), F32)
    for i, total in enumerate([sums[0], sums[1], *totals]):
        packed = jnp.where(row == i, jnp.sum(total, axis=0, keepdims=True), packed)
    packed = jnp.where(row == lane, jnp.sum(packed, axis=1, keepdims=True), 0.0)
    packed = jnp.sum(packed, axis=0, keepdims=True)
    for i in range(out.shape[0]):
        out[i] = packed


def last_kernel(parts, first, second, out):
    total = parts[0]
    for i in range(1, parts.shape[0]):
        total = total + parts[i]
    cross1, square1, along, square2, cross2 = (total[:, i : i + 1] for i in range(5))
    alpha = cross1 / square1
    ratio = along / square1
    weight2 = (cross2 - ratio * cross1) / (square2 - ratio * along)
    weight1 = alpha - ratio * weight2
    for k in range(first.shape[0]):
        out[k] = weight1 * first[k] + weight2 * second[k]


def call(body, operands, outs, scratch=(), specs=None, limit=16 << 20, flops=1 << 22):
    return pl.pallas_call(
        body,
        out_shape=tuple(
            jax.ShapeDtypeStruct(out.shape, out.dtype) if hasattr(out, "dtype") else
            jax.ShapeDtypeStruct(out, F32) for out in outs
        ),
        in_specs=specs or [VMEM] * len(operands),
        out_specs=tuple(VMEM for _ in outs),
        scratch_shapes=tuple(
            pltpu.VMEM(shape, F32) if isinstance(shape, tuple) else shape for shape in scratch
        ),
        compiler_params=pltpu.CompilerParams(vmem_limit_bytes=limit),
        cost_estimate=pl.CostEstimate(flops=flops, bytes_accessed=1 << 20, transcendentals=0),
    )(*operands)


def swap(block, axis, offset):
    count = lax.axis_size(axis)
    pairs = []
    for low in range(offset, count + offset, 2):
        high = (low + 1) % count
        pairs += [(low, high), (high, low)]
    return lax.ppermute(block, axis, pairs)


def exchange(row_near, row_far, col_near, col_far):
    row_far = swap(row_far, GX, 1)
    col_far = swap(col_far, PANEL, 1)
    col_near = swap(col_near, PANEL, 0)
    row_near = swap(row_near, GX, 0)
    return row_near, row_far, col_near, col_far


def sum_over(parts, axes):
    return lax.all_to_all(parts, axes, 0, 0, tiled=True)


def shards(
    right_side, previous, diagonal, vertical, metric_a, metric_b, profile, column_inverse, edge_turn
):
    _, height, width = right_side.shape
    row, col, field = (ROWS, width), (height, width), right_side.shape
    edges = [row, row, col, col]
    turns = jnp.transpose(edge_turn, (0, 2, 1))
    sources = (previous, metric_a, metric_b, diagonal, vertical, right_side, column_inverse)
    loaded = call(
        load_kernel,
        [pltpu.with_memory_space_constraint(x, pltpu.HBM) for x in (turns, profile, *sources)],
        [*sources, row, (8, width), (16, width), *edges],
        [
            pltpu.VMEM(turns.shape, jnp.int32), pltpu.SMEM(profile.shape, F32), row, row,
            pltpu.SemaphoreType.DMA((9,)),
        ],
        specs=[HBM] * 9,
        limit=LOAD_LIMIT,
    )
    previous, metric_a, metric_b, diagonal, vertical, right_side, column_inverse = loaded[:7]
    spread, lanes, flags, *sent = loaded[7:]
    coef = (diagonal, vertical, metric_a, metric_b, spread, lanes, flags)
    got = exchange(*sent)
    resid, search_first, *faces, e0, e1, e2, e3 = call(
        first_kernel,
        (previous, right_side, column_inverse, *coef, *got, *sent),
        [field, field, row, col, *edges],
        [row, row],
    )
    sent = (e0, e1, e2, e3)
    got = exchange(*sent)
    image_first, search_next, part, *sent2 = call(
        second_kernel,
        (search_first, resid, column_inverse, *faces, *coef, *got, *sent),
        [field, field, (2, 8, width), *edges],
        [row, row],
    )
    got = exchange(*sent2)
    plane = lax.axis_size(PLANE)
    depth = lax.axis_size(COLUMN)
    (parts,) = call(
        third_kernel,
        (search_next, resid, image_first, part, *faces, *coef, *got, *sent2),
        [(plane, 1, width)],
        [row, row],
    )
    part = jnp.sum(sum_over(parts, PLANE), axis=0)
    parts = sum_over(jnp.broadcast_to(part[None], (depth, 1, width)), COLUMN)
    (increment,) = call(last_kernel, (parts, search_first, search_next), [field])
    return increment


def solution(mesh):
    finer = Mesh(
        mesh.devices.reshape(SHAPE), ("panel_0", "panel_1", "gx_0", "gx_1", "gx_2")
    )
    spec = P(None, GX, PANEL)
    in_specs = (
        spec, spec, spec, spec, P(GX, PANEL), P(GX, PANEL), P(), P(None, None, GX, PANEL), P(),
    )
    return jax.shard_map(shards, mesh=finer, in_specs=in_specs, out_specs=spec, check_vma=False)
```

time: 116 us -> 100 us (0.86)
  local copies, waits for them, and re-layouts: 11.9 us -> 0.01 us
  starting transfers between devices: 50.8 us -> 45.8 us
  blocking collectives: 35.3 us -> 32.2 us
  waiting for transfers between devices: 9.02 us -> 12.1 us
  Pallas kernels: 8.14 us -> 9.67 us
    unnamed x28 -> x0, local copies, waits for them, and re-layouts: 10.5 us -> none
    ppermute x12, starting transfers between devices: 50.8 us -> 45.8 us  [swap(): return lax.ppermute(block, axis, pairs)]
    ppermute x12, waiting for transfers between devices: 9.02 us -> 12.1 us  [swap(): return lax.ppermute(block, axis, pairs)]
    all_to_all x2, blocking collectives: 35.3 us -> 32.2 us  [sum_over(): return lax.all_to_all(parts, axes, 0, 0, tiled=True)]
    pallas_call x5, Pallas kernels: 8.14 us -> 9.67 us  [call(): pl.pallas_call(body, out_shape=tuple((jax.ShapeDtypeStruct(out.shape, out...]
    pad x2 -> x0, local copies, waits for them, and re-layouts: 1.32 us -> none  [the longest x1 0.66 us: shards(): jnp.pad(profile, (0, width - levels))[None]]
  transfers between devices with their start and end apart: 12 -> 12, of which waited for: 3 -> 3; matrix products, arithmetic and copies ran while one was open for 1% -> 0% of each run, Pallas kernels for 0% -> 0%
where the time goes in v2:
time: 100 us; the launch traced here: 99.9 us
  starting transfers between devices  45.8 us (46%)
  blocking collectives  32.2 us (32%)
  waiting for transfers between devices  12.1 us (12%)
  Pallas kernels  9.67 us (10%)
    ppermute x12, starting transfers between devices, swap(): return lax.ppermute(block, axis, pairs)  45.8 us
    all_to_all x2, blocking collectives, sum_over(): return lax.all_to_all(parts, axes, 0, 0, tiled=True)  32.2 us
    ppermute x12, waiting for transfers between devices, swap(): return lax.ppermute(block, axis, pairs)  12.1 us
    pallas_call x5, Pallas kernels, call(): pl.pallas_call(body, out_shape=tuple((jax.ShapeDtypeStruct(out.shape, out...  9.67 us
  transfers between devices with their start and end apart: 12, of which 3 were waited for; matrix products, arithmetic and copies ran while one was open for 0% of the time, Pallas kernels for 0%

profile of v2, /device:TPU:1, one launch (start us, length us, event | category | flops | bytes accessed | tf_op | source)
XLA Modules:
  0.0 99.9 jit_solution(6640994326986295724)
XLA Ops:
  0.0 2.2 %shard_map.91 = (f32[20,64,128]{2,1,0:T(8,128)S(1)}, f32[64,128]{1,0:T(8,128)S(1)}, f32[64,128]{1,0:T(8,128)S(1)}, f32[20,64,128]{2,1,0:T(8,128)S(1)}, f32[19,64...) custom-call(s32[4,8,64]{2,1,0:T(8,128)} %bitcast.1, ...), custom_call_target="tpu_custom_call" | custom-call | flops 4194304 | bytes 1048576 | tf_op jit(solution)/shard_map/pallas_call | solution.py:271
  2.2 4.0 %collective-permute-start.2 = (f32[64,128]{1,0:T(8,128)S(1)}, f32[64,128]{1,0:T(8,128)S(1)}, u32[]{:S(2)}, u32[]{:S(2)}) collective-permute-start(f32[64,128]{1,0:T(8,128)S(1)} %get-tuple-element.46.refs_13_), channel_id=1, source_target_pairs={{0,64},{64,0},{128,192},{192,128},{256,320},{320,256},{384,448},{4... | collective-permute-start | bytes 98312 | tf_op jit(solution)/shard_map/ppermute | solution.py:293
  6.3 4.7 %collective-permute-start.3 = (f32[64,128]{1,0:T(8,128)S(1)}, f32[64,128]{1,0:T(8,128)S(1)}, u32[]{:S(2)}, u32[]{:S(2)}) collective-permute-start(f32[64,128]{1,0:T(8,128)S(1)} %get-tuple-element.47.refs_14_), channel_id=1, source_target_pairs={{64,128},{128,64},{192,256},{256,192},{320,384},{384,320},{448,0},... | collective-permute-start | bytes 98312 | tf_op jit(solution)/shard_map/ppermute | solution.py:293
  11.0 3.8 %collective-permute-start = (f32[24,128]{1,0:T(8,128)S(1)}, f32[24,128]{1,0:T(8,128)S(1)}, u32[]{:S(2)}, u32[]{:S(2)}) collective-permute-start(f32[24,128]{1,0:T(8,128)S(1)} %get-tuple-element.44.refs_11_), channel_id=1, source_target_pairs={{0,1},{1,0},{2,3},{3,2},{4,5},{5,4},{6,7},{7,6},{8,9},{9,8},{10,11... | collective-permute-start | bytes 36872 | tf_op jit(solution)/shard_map/ppermute | solution.py:293
  14.8 3.6 %collective-permute-start.1 = (f32[24,128]{1,0:T(8,128)S(1)}, f32[24,128]{1,0:T(8,128)S(1)}, u32[]{:S(2)}, u32[]{:S(2)}) collective-permute-start(f32[24,128]{1,0:T(8,128)S(1)} %get-tuple-element.45.refs_12_), channel_id=1, source_target_pairs={{1,2},{2,1},{3,4},{4,3},{5,6},{6,5},{7,8},{8,7},{9,10},{10,9},{11,... | collective-permute-start | bytes 36872 | tf_op jit(solution)/shard_map/ppermute | solution.py:293
  18.4 0.0 collective-permute-done.refs_7_
  18.4 2.9 %collective-permute-done.1.refs_8_ = f32[24,128]{1,0:T(8,128)S(1)} collective-permute-done((f32[24,128]{1,0:T(8,128)S(1)}, f32[24,128]{1,0:T(8,128)S(1)}, u32[]{:S(2)}, u32[]{:S(2)}) %collective-permute-start.1) | collective-permute-done | bytes 12320 | tf_op jit(solution)/shard_map/ppermute | solution.py:293
  21.4 2.2 %shard_map.92 = (f32[20,64,128]{2,1,0:T(8,128)S(1)}, f32[20,64,128]{2,1,0:T(8,128)S(1)}, f32[24,128]{1,0:T(8,128)S(1)}, f32[64,128]{1,0:T(8,128)S(1)}, f32[24,12...) custom-call(f32[20,64,128]{2,1,0:T(8,128)S(1)} %get-tuple-element.34.field, ...), custom_call_target="tpu_custom_call" | custom-call | flops 4194304 | bytes 1048576 | tf_op jit(solution)/shard_map/pallas_call | solution.py:271
  23.6 3.6 %collective-permute-start.6 = (f32[64,128]{1,0:T(8,128)S(1)}, f32[64,128]{1,0:T(8,128)S(1)}, u32[]{:S(2)}, u32[]{:S(2)}) collective-permute-start(f32[64,128]{1,0:T(8,128)S(1)} %get-tuple-element.54.refs_13_), channel_id=1, source_target_pairs={{0,64},{64,0},{128,192},{192,128},{256,320},{320,256},{384,448},{4... | collective-permute-start | bytes 98312 | tf_op jit(solution)/shard_map/ppermute | solution.py:293
  27.2 4.0 %collective-permute-start.7 = (f32[64,128]{1,0:T(8,128)S(1)}, f32[64,128]{1,0:T(8,128)S(1)}, u32[]{:S(2)}, u32[]{:S(2)}) collective-permute-start(f32[64,128]{1,0:T(8,128)S(1)} %get-tuple-element.55.refs_14_), channel_id=1, source_target_pairs={{64,128},{128,64},{192,256},{256,192},{320,384},{384,320},{448,0},... | collective-permute-start | bytes 98312 | tf_op jit(solution)/shard_map/ppermute | solution.py:293
  31.3 6.7 %collective-permute-start.4 = (f32[24,128]{1,0:T(8,128)S(1)}, f32[24,128]{1,0:T(8,128)S(1)}, u32[]{:S(2)}, u32[]{:S(2)}) collective-permute-start(f32[24,128]{1,0:T(8,128)S(1)} %get-tuple-element.52.refs_11_), channel_id=1, source_target_pairs={{0,1},{1,0},{2,3},{3,2},{4,5},{5,4},{6,7},{7,6},{8,9},{9,8},{10,11... | collective-permute-start | bytes 36872 | tf_op jit(solution)/shard_map/ppermute | solution.py:293
  37.9 1.9 %collective-permute-start.5 = (f32[24,128]{1,0:T(8,128)S(1)}, f32[24,128]{1,0:T(8,128)S(1)}, u32[]{:S(2)}, u32[]{:S(2)}) collective-permute-start(f32[24,128]{1,0:T(8,128)S(1)} %get-tuple-element.53.refs_12_), channel_id=1, source_target_pairs={{1,2},{2,1},{3,4},{4,3},{5,6},{6,5},{7,8},{8,7},{9,10},{10,9},{11,... | collective-permute-start | bytes 36872 | tf_op jit(solution)/shard_map/ppermute | solution.py:293
  39.9 4.6 %collective-permute-done.5.refs_8_ = f32[24,128]{1,0:T(8,128)S(1)} collective-permute-done((f32[24,128]{1,0:T(8,128)S(1)}, f32[24,128]{1,0:T(8,128)S(1)}, u32[]{:S(2)}, u32[]{:S(2)}) %collective-permute-start.5) | collective-permute-done | bytes 12320 | tf_op jit(solution)/shard_map/ppermute | solution.py:293
  44.5 2.2 %shard_map.93 = (f32[20,64,128]{2,1,0:T(8,128)S(1)}, f32[20,64,128]{2,1,0:T(8,128)S(1)}, f32[2,8,128]{2,1,0:T(8,128)S(1)}, f32[24,128]{1,0:T(8,128)S(1)}, f32[24...) custom-call(f32[20,64,128]{2,1,0:T(8,128)S(1)} %get-tuple-element.48.field.first, ...), custom_call_target="tpu_custom_call" | custom-call | flops 4194304 | bytes 1048576 | tf_op jit(solution)/shard_map/pallas_call | solution.py:271
  46.7 3.4 %collective-permute-start.10 = (f32[64,128]{1,0:T(8,128)S(1)}, f32[64,128]{1,0:T(8,128)S(1)}, u32[]{:S(2)}, u32[]{:S(2)}) collective-permute-start(f32[64,128]{1,0:T(8,128)S(1)} %get-tuple-element.61.refs_13_), channel_id=1, source_target_pairs={{0,64},{64,0},{128,192},{192,128},{256,320},{320,256},{384,448},{4... | collective-permute-start | bytes 98312 | tf_op jit(solution)/shard_map/ppermute | solution.py:293
  50.1 3.6 %collective-permute-start.11 = (f32[64,128]{1,0:T(8,128)S(1)}, f32[64,128]{1,0:T(8,128)S(1)}, u32[]{:S(2)}, u32[]{:S(2)}) collective-permute-start(f32[64,128]{1,0:T(8,128)S(1)} %get-tuple-element.62.refs_14_), channel_id=1, source_target_pairs={{64,128},{128,64},{192,256},{256,192},{320,384},{384,320},{448,0},... | collective-permute-start | bytes 98312 | tf_op jit(solution)/shard_map/ppermute | solution.py:293
  53.7 4.4 %collective-permute-start.8 = (f32[24,128]{1,0:T(8,128)S(1)}, f32[24,128]{1,0:T(8,128)S(1)}, u32[]{:S(2)}, u32[]{:S(2)}) collective-permute-start(f32[24,128]{1,0:T(8,128)S(1)} %get-tuple-element.59.refs_11_), channel_id=1, source_target_pairs={{0,1},{1,0},{2,3},{3,2},{4,5},{5,4},{6,7},{7,6},{8,9},{9,8},{10,11... | collective-permute-start | bytes 36872 | tf_op jit(solution)/shard_map/ppermute | solution.py:293
  58.1 1.9 %collective-permute-start.9 = (f32[24,128]{1,0:T(8,128)S(1)}, f32[24,128]{1,0:T(8,128)S(1)}, u32[]{:S(2)}, u32[]{:S(2)}) collective-permute-start(f32[24,128]{1,0:T(8,128)S(1)} %get-tuple-element.60.refs_12_), channel_id=1, source_target_pairs={{1,2},{2,1},{3,4},{4,3},{5,6},{6,5},{7,8},{8,7},{9,10},{10,9},{11,... | collective-permute-start | bytes 36872 | tf_op jit(solution)/shard_map/ppermute | solution.py:293
  60.1 4.6 %collective-permute-done.9.refs_8_ = f32[24,128]{1,0:T(8,128)S(1)} collective-permute-done((f32[24,128]{1,0:T(8,128)S(1)}, f32[24,128]{1,0:T(8,128)S(1)}, u32[]{:S(2)}, u32[]{:S(2)}) %collective-permute-start.9) | collective-permute-done | bytes 12320 | tf_op jit(solution)/shard_map/ppermute | solution.py:293
  64.7 1.7 %shard_map.94 = f32[32,1,128]{2,1,0:T(1,128)S(1)} custom-call(f32[20,64,128]{2,1,0:T(8,128)S(1)} %get-tuple-element.56.field.second, f32[20,64,128]{2,1,0:T(8,128)S(1)} %get-tuple-element.49.resid, f32[20,64,128]{2,1,0:T(8,128)S(1)} %get-tuple-element.57.first, f32[2,8,128]{2,1,0:T(8,128)S(1)} %get-tuple-element.58.sums, ...), custom_call_target="tpu_custom_call" | custom-call | flops 4194304 | bytes 1048576 | tf_op jit(solution)/shard_map/pallas_call | solution.py:271
  66.4 12.6 %all_to_all.10 = f32[32,1,128]{2,1,0:T(1,128)S(1)} all-to-all(f32[32,1,128]{2,1,0:T(1,128)S(1)} %shard_map.94), channel_id=1, replica_groups=mesh['panel_0'=2,'panel_1'=4,'gx_0'=16,'gx_1'=2,'gx_2'=2] {'panel_0','pa..., dimensions={0} | all-to-all | bytes 32768 | tf_op jit(solution)/shard_map/all_to_all | solution.py:305
  78.9 0.1 reduce_sum.9
  79.0 19.6 %all_to_all.11.parts = f32[16,1,128]{2,1,0:T(1,128)S(1)} all-to-all(f32[16,1,128]{2,1,0:T(1,128)S(1)} %broadcast_in_dim.2), channel_id=1, replica_groups=mesh['panel_0'=2,'panel_1'=4,'gx_0'=16,'gx_1'=2,'gx_2'=2] {'gx_0'}, dimensions={0} | all-to-all | bytes 16384 | tf_op jit(solution)/shard_map/all_to_all | solution.py:305
  98.6 1.3 %shard_map.95 = f32[20,64,128]{2,1,0:T(8,128)} custom-call(f32[16,1,128]{2,1,0:T(1,128)S(1)} %all_to_all.11.parts, f32[20,64,128]{2,1,0:T(8,128)S(1)} %get-tuple-element.48.field.first, f32[20,64,128]{2,1,0:T(8,128)S(1)} %get-tuple-element.56.field.second), custom_call_target="tpu_custom_call" | custom-call | flops 4194304 | bytes 1048576 | tf_op jit(solution)/shard_map/pallas_call | solution.py:271
  (9 shorter events, 0.0 us)
Async XLA Ops:
  2.2 19.1 %collective-permute-start.2 = (f32[64,128]{1,0:T(8,128)S(1)}, f32[64,128]{1,0:T(8,128)S(1)}, u32[]{:S(2)}, u32[]{:S(2)}) collective-permute-start(f32[64,128]{1,0:T(8,128)S(1)} %get-tuple-element.46.refs_13_), channel_id=1, source_target_pairs={{0,64},{64,0},{128,192},{192,128},{256,320},{320,256},{384,448},{4... | collective-permute-start | bytes 98312 | tf_op jit(solution)/shard_map/ppermute | solution.py:293
  6.3 15.1 %collective-permute-start.3 = (f32[64,128]{1,0:T(8,128)S(1)}, f32[64,128]{1,0:T(8,128)S(1)}, u32[]{:S(2)}, u32[]{:S(2)}) collective-permute-start(f32[64,128]{1,0:T(8,128)S(1)} %get-tuple-element.47.refs_14_), channel_id=1, source_target_pairs={{64,128},{128,64},{192,256},{256,192},{320,384},{384,320},{448,0},... | collective-permute-start | bytes 98312 | tf_op jit(solution)/shard_map/ppermute | solution.py:293
  11.0 7.4 %collective-permute-start = (f32[24,128]{1,0:T(8,128)S(1)}, f32[24,128]{1,0:T(8,128)S(1)}, u32[]{:S(2)}, u32[]{:S(2)}) collective-permute-start(f32[24,128]{1,0:T(8,128)S(1)} %get-tuple-element.44.refs_11_), channel_id=1, source_target_pairs={{0,1},{1,0},{2,3},{3,2},{4,5},{5,4},{6,7},{7,6},{8,9},{9,8},{10,11... | collective-permute-start | bytes 36872 | tf_op jit(solution)/shard_map/ppermute | solution.py:293
  14.8 6.5 %collective-permute-start.1 = (f32[24,128]{1,0:T(8,128)S(1)}, f32[24,128]{1,0:T(8,128)S(1)}, u32[]{:S(2)}, u32[]{:S(2)}) collective-permute-start(f32[24,128]{1,0:T(8,128)S(1)} %get-tuple-element.45.refs_12_), channel_id=1, source_target_pairs={{1,2},{2,1},{3,4},{4,3},{5,6},{6,5},{7,8},{8,7},{9,10},{10,9},{11,... | collective-permute-start | bytes 36872 | tf_op jit(solution)/shard_map/ppermute | solution.py:293
  23.6 20.9 %collective-permute-start.6 = (f32[64,128]{1,0:T(8,128)S(1)}, f32[64,128]{1,0:T(8,128)S(1)}, u32[]{:S(2)}, u32[]{:S(2)}) collective-permute-start(f32[64,128]{1,0:T(8,128)S(1)} %get-tuple-element.54.refs_13_), channel_id=1, source_target_pairs={{0,64},{64,0},{128,192},{192,128},{256,320},{320,256},{384,448},{4... | collective-permute-start | bytes 98312 | tf_op jit(solution)/shard_map/ppermute | solution.py:293
  27.2 17.2 %collective-permute-start.7 = (f32[64,128]{1,0:T(8,128)S(1)}, f32[64,128]{1,0:T(8,128)S(1)}, u32[]{:S(2)}, u32[]{:S(2)}) collective-permute-start(f32[64,128]{1,0:T(8,128)S(1)} %get-tuple-element.55.refs_14_), channel_id=1, source_target_pairs={{64,128},{128,64},{192,256},{256,192},{320,384},{384,320},{448,0},... | collective-permute-start | bytes 98312 | tf_op jit(solution)/shard_map/ppermute | solution.py:293
  31.3 8.6 %collective-permute-start.4 = (f32[24,128]{1,0:T(8,128)S(1)}, f32[24,128]{1,0:T(8,128)S(1)}, u32[]{:S(2)}, u32[]{:S(2)}) collective-permute-start(f32[24,128]{1,0:T(8,128)S(1)} %get-tuple-element.52.refs_11_), channel_id=1, source_target_pairs={{0,1},{1,0},{2,3},{3,2},{4,5},{5,4},{6,7},{7,6},{8,9},{9,8},{10,11... | collective-permute-start | bytes 36872 | tf_op jit(solution)/shard_map/ppermute | solution.py:293
  37.9 6.5 %collective-permute-start.5 = (f32[24,128]{1,0:T(8,128)S(1)}, f32[24,128]{1,0:T(8,128)S(1)}, u32[]{:S(2)}, u32[]{:S(2)}) collective-permute-start(f32[24,128]{1,0:T(8,128)S(1)} %get-tuple-element.53.refs_12_), channel_id=1, source_target_pairs={{1,2},{2,1},{3,4},{4,3},{5,6},{6,5},{7,8},{8,7},{9,10},{10,9},{11,... | collective-permute-start | bytes 36872 | tf_op jit(solution)/shard_map/ppermute | solution.py:293
  46.7 18.0 %collective-permute-start.10 = (f32[64,128]{1,0:T(8,128)S(1)}, f32[64,128]{1,0:T(8,128)S(1)}, u32[]{:S(2)}, u32[]{:S(2)}) collective-permute-start(f32[64,128]{1,0:T(8,128)S(1)} %get-tuple-element.61.refs_13_), channel_id=1, source_target_pairs={{0,64},{64,0},{128,192},{192,128},{256,320},{320,256},{384,448},{4... | collective-permute-start | bytes 98312 | tf_op jit(solution)/shard_map/ppermute | solution.py:293
  50.1 14.6 %collective-permute-start.11 = (f32[64,128]{1,0:T(8,128)S(1)}, f32[64,128]{1,0:T(8,128)S(1)}, u32[]{:S(2)}, u32[]{:S(2)}) collective-permute-start(f32[64,128]{1,0:T(8,128)S(1)} %get-tuple-element.62.refs_14_), channel_id=1, source_target_pairs={{64,128},{128,64},{192,256},{256,192},{320,384},{384,320},{448,0},... | collective-permute-start | bytes 98312 | tf_op jit(solution)/shard_map/ppermute | solution.py:293
  53.7 6.4 %collective-permute-start.8 = (f32[24,128]{1,0:T(8,128)S(1)}, f32[24,128]{1,0:T(8,128)S(1)}, u32[]{:S(2)}, u32[]{:S(2)}) collective-permute-start(f32[24,128]{1,0:T(8,128)S(1)} %get-tuple-element.59.refs_11_), channel_id=1, source_target_pairs={{0,1},{1,0},{2,3},{3,2},{4,5},{5,4},{6,7},{7,6},{8,9},{9,8},{10,11... | collective-permute-start | bytes 36872 | tf_op jit(solution)/shard_map/ppermute | solution.py:293
  58.1 6.5 %collective-permute-start.9 = (f32[24,128]{1,0:T(8,128)S(1)}, f32[24,128]{1,0:T(8,128)S(1)}, u32[]{:S(2)}, u32[]{:S(2)}) collective-permute-start(f32[24,128]{1,0:T(8,128)S(1)} %get-tuple-element.60.refs_12_), channel_id=1, source_target_pairs={{1,2},{2,1},{3,4},{4,3},{5,6},{6,5},{7,8},{8,7},{9,10},{10,9},{11,... | collective-permute-start | bytes 36872 | tf_op jit(solution)/shard_map/ppermute | solution.py:293
